TPU v7x, 256 devices: a whole 4x4x8 slice. The times are simulated.
256 devices in a mesh: blk: 128 (over x, z, y_lo, core), mp: 2 (over y_hi).
Axes of the slice: x: 4, y: 4 (y_hi: 2, y_lo: 2; y = y_hi * 2 + y_lo), z: 8, core: 2. Of those that a mesh axis runs over, the one named last changes fastest.
Arguments:
- features: bfloat16 [128, 2, 2, 256, 1280], P('blk', None, None, None, 'mp'), may hold values from -62 to 62
- w_query: bfloat16 [1280, 1280], P(None, 'mp'), may hold values from -2 to 2
- w_key: bfloat16 [1280, 1280], P(None, 'mp'), may hold values from -2 to 2
- w_value: bfloat16 [1280, 1280], P(None, 'mp'), may hold values from -0.15625 to 0.15625
- w_out: bfloat16 [1280, 1280], P('mp'), may hold values from -0.15625 to 0.15625
- w_head: bfloat16 [1280, 64], replicated, may hold values from -0.15625 to 0.15625
- offsets: int32 [128], P('blk'), may hold values from 0 to 2047, as said below
- blend_mask: int32 [128, 64, 64], P('blk'), may hold values from 1 to 4
Outputs:
- panorama: float32 [2, 2048, 256], P(None, 'blk')
Inputs may be any that keep to these rules, and one draw needn't show every extreme that they name: offsets[w] = 16 * w + s for one s shared by all windows, 0 <= s < 16.
All inputs are finite; a program needn't handle non-finite values.
Results may differ from a plain program's by a relative error of at most 0.0064.
Values may be sent and summed in bfloat16 or wider, within the bound.
A program may use at most 64 MiB of HBM per device.

v0:
```python
import jax
import jax.numpy as jnp
from jax import lax
from jax.sharding import PartitionSpec as P

HEAD = 64
GRID = 16
PATCH = 4
CHAN = 4
STRIDE = 16
WINDOW = 64
OUTW = 64


guidance = 3.0


def laid_out(pieces, dim):
    pieces = jnp.moveaxis(pieces, 0, dim)
    dims = pieces.shape
    return pieces.reshape(*dims[:dim], dims[dim] * dims[dim + 1], *dims[dim + 2 :])


def from_everyone(x, axis):
    count = lax.axis_size(axis)
    return lax.all_to_all(jnp.broadcast_to(x[None], (count, *x.shape)), axis, 0, 0, tiled=True)


def gathered_copies(x, axis, dim):
    return laid_out(from_everyone(x, axis), dim)


def over_pieces(x, axis):
    pieces = lax.all_gather(x, axis).astype(jnp.float32)
    return pieces.sum(axis=0)


def shifted(x, axis, by):
    count = lax.axis_size(axis)
    return lax.ppermute(x, axis, [(i, (i + by) % count) for i in range(count)])


def shards(features, w_query, w_key, w_value, w_out, w_head, offsets, blend_mask):
    gathered = gathered_copies(features, "mp", 4)
    batch_count = gathered.shape[1]
    token_count = gathered.shape[3]
    model_width = gathered.shape[4]
    sequences = batch_count * 2
    local_heads = w_query.shape[1] // HEAD
    token_plain = gathered.reshape(-1, model_width)
    token_rows = token_plain.astype(jnp.float32)
    row_mean = jnp.mean(token_rows, axis=1, keepdims=True)
    centred = token_rows - row_mean
    row_var = jnp.mean(centred * centred, axis=1, keepdims=True)
    normed = (centred * lax.rsqrt(row_var + 1e-05)).astype(jnp.bfloat16)
    queries = (
        jnp.dot(normed, w_query, preferred_element_type=jnp.float32)
        .astype(jnp.bfloat16)
        .reshape(sequences, token_count, local_heads, HEAD)
    )
    key_rows = (
        jnp.dot(normed, w_key, preferred_element_type=jnp.float32)
        .astype(jnp.bfloat16)
        .reshape(sequences, token_count, local_heads, HEAD)
    )
    value_rows = (
        jnp.dot(normed, w_value, preferred_element_type=jnp.float32)
        .astype(jnp.bfloat16)
        .reshape(sequences, token_count, local_heads, HEAD)
    )
    scores = (
        jnp.einsum("sqhd,skhd->shqk", queries, key_rows, preferred_element_type=jnp.float32)
        / HEAD**0.5
    )
    scores = scores - jnp.max(scores, axis=3, keepdims=True)
    expont = jnp.exp(scores)
    attend = (expont / jnp.sum(expont, axis=3, keepdims=True)).astype(jnp.bfloat16)
    context = jnp.einsum(
        "shqk,skhd->sqhd", attend, value_rows, preferred_element_type=jnp.float32
    ).astype(jnp.bfloat16)
    context = context.reshape(-1, local_heads * HEAD)
    partial_value = jnp.dot(context, w_out, preferred_element_type=jnp.float32)
    head_weight = w_head.astype(jnp.float32)
    head_part = jnp.dot(partial_value, head_weight, precision=lax.Precision.HIGHEST)
    tok_out = over_pieces(head_part.astype(jnp.bfloat16), "mp").astype(jnp.float32) + jnp.dot(
        token_plain, w_head, preferred_element_type=jnp.float32
    )
    tok_out = tok_out.reshape(batch_count, 2, token_count, OUTW)
    guided = tok_out[:, 0] + guidance * (tok_out[:, 1] - tok_out[:, 0])
    spread = guided.reshape(batch_count, GRID, GRID, PATCH, PATCH, CHAN).transpose(0, 2, 3, 1, 4, 5)
    spread = spread.reshape(batch_count, WINDOW, WINDOW * CHAN)
    weight = blend_mask[0].astype(jnp.float32)
    weighted = spread * jnp.repeat(weight, CHAN, axis=1)[None]
    shift_cols = offsets[0] - STRIDE * lax.axis_index("blk")
    zero_index = jnp.zeros((), jnp.int32)
    frame_num = lax.dynamic_update_slice(
        jnp.zeros((batch_count, WINDOW + STRIDE, WINDOW * CHAN), jnp.float32),
        weighted,
        (zero_index, shift_cols, zero_index),
    )
    frame_weight = lax.dynamic_update_slice(
        jnp.zeros((WINDOW + STRIDE, WINDOW), jnp.float32), weight, (shift_cols, zero_index)
    )
    piece_count = WINDOW // STRIDE + 1
    numerators = [frame_num[:, j * STRIDE : (j + 1) * STRIDE] for j in range(piece_count)]
    weight_pieces = [frame_weight[j * STRIDE : (j + 1) * STRIDE] for j in range(piece_count)]
    for bit_level in range(piece_count.bit_length()):
        distance = 1 << bit_level
        sources = [j for j in range(piece_count) if j % (2 * distance) == distance]
        arrived = shifted(
            (
                jnp.stack([numerators[j] for j in sources]),
                jnp.stack([weight_pieces[j] for j in sources]),
            ),
            "blk",
            distance,
        )
        for i, j in enumerate(sources):
            numerators[j - distance] = numerators[j - distance] + arrived[0][i]
            weight_pieces[j - distance] = weight_pieces[j - distance] + arrived[1][i]
    blended_num = numerators[0]
    blended_weight = weight_pieces[0]
    return blended_num / jnp.repeat(blended_weight, CHAN, axis=1)[None]


def solution(mesh):
    return jax.shard_map(
        shards,
        mesh=mesh,
        in_specs=(
            P("blk", None, None, None, "mp"),
            P(None, "mp"),
            P(None, "mp"),
            P(None, "mp"),
            P("mp", None),
            P(),
            P("blk"),
            P("blk", None, None),
        ),
        out_specs=P(None, "blk", None),
        check_vma=False,
    )
```

profile of v0, /device:TPU:8, one launch (start us, length us, event | category | flops | bytes accessed | tf_op | source)
XLA Modules:
  0.0 141.1 jit_solution(2092865525335409924)
XLA Ops:
  0.0 3.2 %broadcast_in_dim.26 = bf16[2,1,2,2,256,640]{5,4,3,2,1,0:T(8,128)(2,1)} broadcast(bf16[2,2,256,640]{3,2,1,0:T(8,128)(2,1)} %bitcast.120), dimensions={2,3,4,5} | broadcast | bytes 3932160 | tf_op jit(solution)/shard_map/broadcast_in_dim | solution.py:26
  3.2 5.2 %all-to-all-start = ((bf16[2,1,2,2,256,640]{5,4,3,2,1,0:T(8,128)(2,1)}), bf16[2,1,2,2,256,640]{5,4,3,2,1,0:T(8,128)(2,1)}, u32[]{:S(2)}, u32[]{:S(2)}) async-start(bf16[2,1,2,2,256,640]{5,4,3,2,1,0:T(8,128)(2,1)} %broadcast_in_dim.26), calls=%async_computation | async-start | bytes 5242880 | tf_op jit(solution)/shard_map/all_to_all | solution.py:26
  9.0 0.3 dynamic_update_slice.7
  9.5 31.3 %all-to-all-done = bf16[2,1,2,2,256,640]{5,4,3,2,1,0:T(8,128)(2,1)} async-done(((bf16[2,1,2,2,256,640]{5,4,3,2,1,0:T(8,128)(2,1)}), bf16[2,1,2,2,256,640]{5,4,3,2,1,0:T(8,128)(2,1)}, u32[]{:S(2)}, u32[]{:S(2)}) %all-to-all-start) | async-done | bytes 2621472 | tf_op jit(solution)/shard_map/all_to_all | solution.py:26
  40.8 2.2 %convert_reduce_fusion = f32[2,2,256]{2,1,0:T(2,128)S(1)} fusion(bf16[2,1,2,2,256,640]{5,4,3,2,1,0:T(8,128)(2,1)} %all-to-all-done), kind=kLoop, calls=%fused_computation.6 | loop fusion | flops 2620416 | bytes 2625536 | tf_op jit(solution)/shard_map/reduce_sum | solution.py:52
  43.0 2.6 %fusion.5 = f32[2,2,256]{2,1,0:T(2,128)S(1)} fusion(f32[2,2,256]{2,1,0:T(2,128)S(1)} %get-tuple-element.16, bf16[2,1,2,2,256,640]{5,4,3,2,1,0:T(8,128)(2,1)} %all-to-all-done), kind=kLoop, calls=%fused_computation.8 | loop fusion | flops 5241856 | bytes 2629632 | tf_op jit(solution)/shard_map/reduce_sum | solution.py:54
  45.6 4.4 %copy.43 = bf16[1,2,2,256,2,640]{5,4,3,2,1,0:T(2,128)(2,1)S(1)} copy(bf16[1,2,2,256,2,640]{5,3,2,1,0,4:T(8,128)(2,1)} %bitcast.1) | data formatting | bytes 5242880 | tf_op jit(solution)/shard_map/transpose | solution.py:19
  50.0 0.5 copy.62
  50.6 1.5 %copy-done.1 = bf16[128,8,2,640]{3,1,2,0:T(8,128)(2,1)} copy-done((bf16[128,8,2,640]{3,1,2,0:T(8,128)(2,1)}, bf16[128,8,2,640]{3,1,2,0:T(8,128)(2,1)S(1)}, u32[]{:S(2)}) %copy-start.1) | copy-done | bytes 2621464
  52.1 2.3 %convolution_convert_fusion.1 = bf16[1024,640]{1,0:T(8,128)(2,1)S(1)} fusion(bf16[1280,640]{1,0:T(8,128)(2,1)S(1)} %copy-done.4, bf16[1024,1280]{1,0:T(8,128)(2,1)S(1)} %bitcast.113, f32[1024]{0:T(1024)S(1)} %bitcast.123, f32[1024]{0:T(1024)S(1)} %bitcast.126), kind=kOutput, calls=%fused_computation.14 | convolution fusion | flops 1683619840 | bytes 5578752 | tf_op jit(solution)/shard_map/dot_general | solution.py:57
  54.4 1.7 %copy.45 = bf16[1024,640]{0,1:T(8,128)(2,1)} copy(bf16[1024,640]{1,0:T(8,128)(2,1)S(1)} %convolution_convert_fusion.1) | data formatting | bytes 2621440 | tf_op jit(solution)/shard_map/convert_element_type | solution.py:58
  56.1 2.9 %reshape.64 = bf16[4,256,10,64]{1,0,3,2:T(4,128)(2,1)S(1)} reshape(bf16[1024,640]{0,1:T(8,128)(2,1)} %copy.45) | data formatting | bytes 2621440 | tf_op jit(solution)/shard_map/reshape | solution.py:59
  59.0 5.5 %convolution_convert_fusion = bf16[1024,640]{1,0:T(8,128)(2,1)} fusion(bf16[1280,640]{1,0:T(8,128)(2,1)} %param.10, bf16[1024,1280]{1,0:T(8,128)(2,1)} %bitcast.114, f32[1024]{0:T(1024)S(1)} %bitcast.124, f32[1024]{0:T(1024)S(1)} %bitcast.127), kind=kOutput, calls=%fused_computation.13 | convolution fusion | flops 1683619840 | bytes 5578752 | tf_op jit(solution)/shard_map/dot_general | solution.py:62
  64.6 2.5 %copy.46 = bf16[1024,640]{0,1:T(8,128)(2,1)} copy(bf16[1024,640]{1,0:T(8,128)(2,1)} %convolution_convert_fusion) | data formatting | bytes 2621440 | tf_op jit(solution)/shard_map/convert_element_type | solution.py:63
  67.1 3.8 %reshape.65 = bf16[4,256,10,64]{1,0,3,2:T(4,128)(2,1)} reshape(bf16[1024,640]{0,1:T(8,128)(2,1)} %copy.46) | data formatting | bytes 2621440 | tf_op jit(solution)/shard_map/reshape | solution.py:64
  70.8 2.9 %fusion.11 = f32[4,10,256,256]{2,3,1,0:T(8,128)S(1)} fusion(bf16[4,256,10,64]{1,0,3,2:T(4,128)(2,1)} %reshape.65, bf16[4,256,10,64]{1,0,3,2:T(4,128)(2,1)S(1)} %reshape.64), kind=kOutput, calls=%fused_computation.18 | convolution fusion | flops 335544320 | bytes 13107200 | tf_op jit(solution)/shard_map/sqhd,skhd->shqk/dot_general | solution.py:72
  73.7 5.4 %fusion.28 = (f32[4,10,256]{2,1,0:T(8,128)S(1)}, f32[4,10,256,256]{2,3,1,0:T(8,128)}) fusion(f32[4,10,256,256]{2,3,1,0:T(8,128)S(1)} %fusion.11), kind=kOutput, calls=%fused_computation.54 | output fusion | flops 10486015 | bytes 21012480 | tf_op jit(solution)/shard_map/sub | solution.py:75
  79.2 5.1 %convolution_convert_fusion.2 = bf16[1024,640]{1,0:T(8,128)(2,1)} fusion(bf16[1280,640]{1,0:T(8,128)(2,1)S(1)} %copy-done.5, bf16[1024,1280]{1,0:T(8,128)(2,1)} %bitcast.115, f32[1024]{0:T(1024)S(1)} %bitcast.125, f32[1024]{0:T(1024)S(1)} %bitcast.128), kind=kOutput, calls=%fused_computation.15 | convolution fusion | flops 1683619840 | bytes 5578752 | tf_op jit(solution)/shard_map/dot_general | solution.py:67
  84.2 1.6 %copy.44 = bf16[1024,640]{0,1:T(8,128)(2,1)S(1)} copy(bf16[1024,640]{1,0:T(8,128)(2,1)} %convolution_convert_fusion.2) | data formatting | bytes 2621440 | tf_op jit(solution)/shard_map/convert_element_type | solution.py:68
  85.8 1.9 %reshape.63 = bf16[4,256,10,64]{1,0,3,2:T(4,128)(2,1)} reshape(bf16[1024,640]{0,1:T(8,128)(2,1)S(1)} %copy.44) | data formatting | bytes 2621440 | tf_op jit(solution)/shard_map/reshape | solution.py:69
  87.7 5.3 %fusion.9 = bf16[4,256,10,64]{1,3,2,0:T(8,128)(2,1)S(1)} fusion(f32[4,10,256,256]{2,3,1,0:T(8,128)} %get-tuple-element.18, f32[4,10,256]{2,1,0:T(8,128)S(1)} %get-tuple-element.17, bf16[4,256,10,64]{1,0,3,2:T(4,128)(2,1)} %reshape.63), kind=kOutput, calls=%fused_computation.16 | convolution fusion | flops 341442560 | bytes 13148160 | tf_op jit(solution)/shard_map/shqk,skhd->sqhd/dot_general | solution.py:78
  93.0 1.0 copy.51
  94.1 0.3 copy.65
  94.4 2.3 %fusion.29 = f32[1024,1280]{1,0:T(8,128)S(1)} fusion(bf16[1024,640]{0,1:T(8,128)(2,1)S(1)} %bitcast.119, bf16[640,1280]{1,0:T(8,128)(2,1)S(1)} %copy-done), kind=kOutput, calls=%fused_computation.55 | convolution fusion | flops 1677721600 | bytes 8192000 | tf_op jit(solution)/shard_map/dot_general | solution.py:82
  96.7 2.8 %convolution_convert_fusion.3 = bf16[1024,64]{0,1:T(8,128)(2,1)S(1)} fusion(f32[1024,1280]{1,0:T(8,128)S(1)} %fusion.29, bf16[1280,64]{0,1:T(8,128)(2,1)S(1)} %copy-done.2), kind=kOutput, calls=%fused_computation.22 | convolution fusion | flops 1006698496 | bytes 5537792 | tf_op jit(solution)/shard_map/dot_general | solution.py:84
  99.5 7.1 %all-gather = bf16[2048,64]{0,1:T(8,128)(2,1)S(1)} all-gather(bf16[1024,64]{0,1:T(8,128)(2,1)S(1)} %convolution_convert_fusion.3), channel_id=2, replica_groups=mesh['blk'=128,'mp'=2] {'mp'}, dimensions={0}, use_global_device_ids=true | all-gather | bytes 393216 | tf_op jit(solution)/shard_map/all_gather | solution.py:34
  106.6 0.5 reshape.70
  107.2 0.6 reduce_sum.39
  107.8 2.6 %convolution_add_fusion = f32[1024,64]{0,1:T(8,128)S(1)} fusion(f32[1024,64]{0,1:T(8,128)S(1)} %reduce_sum.39, bf16[1024,1280]{1,0:T(8,128)(2,1)} %bitcast.116, bf16[1280,64]{0,1:T(8,128)(2,1)S(1)} %copy-done.2), kind=kOutput, calls=%fused_computation.21 | convolution fusion | flops 167837696 | bytes 3309568 | tf_op jit(solution)/shard_map/dot_general | solution.py:85
  110.4 0.2 reshape.67
  110.7 0.2 fusion.27
  110.9 1.3 squeeze.35
  112.2 1.4 squeeze.36
  113.6 1.7 %add_bitcast_fusion = f32[2,16,4,16,4,4]{1,3,5,4,2,0:T(8,128)S(1)} fusion(f32[2,16,16,4,4,4]{2,1,5,4,3,0:T(8,128)} %squeeze.35, f32[2,16,16,4,4,4]{2,1,5,4,3,0:T(8,128)} %squeeze.36), kind=kLoop, calls=%fused_computation.23 | loop fusion | flops 98304 | bytes 393216 | tf_op jit(solution)/shard_map/transpose | solution.py:90
  115.3 4.5 %copy.54 = f32[2,16,4,16,4,4]{2,1,5,4,3,0:T(8,128)} copy(f32[2,16,4,16,4,4]{1,3,5,4,2,0:T(8,128)S(1)} %add_bitcast_fusion) | data formatting | bytes 262144 | tf_op jit(solution)/shard_map/transpose | solution.py:90
  119.8 3.6 %reshape.68 = f32[2,64,256]{1,2,0:T(8,128)S(1)} reshape(f32[2,16,4,16,4,4]{2,1,5,4,3,0:T(8,128)} %copy.54) | data formatting | bytes 262144 | tf_op jit(solution)/shard_map/reshape | solution.py:91
  123.5 0.1 copy.56
  123.7 0.4 dynamic_update_slice.6
  124.1 0.3 collective-permute-start
  124.5 1.9 %collective-permute-start.4 = (f32[1,16,64]{2,1,0:T(8,128)S(1)}, f32[1,16,64]{2,1,0:T(8,128)S(1)}, u32[]{:S(2)}, u32[]{:S(2)}) collective-permute-start(f32[1,16,64]{2,1,0:T(8,128)S(1)} %get-tuple-element.11), channel_id=1, source_target_pairs={{0,4},{2,6},{4,8},{6,10},{8,12},{10,14},{12,16},{14,18},{16,20},{1... | collective-permute-start | bytes 12296 | tf_op jit(solution)/shard_map/ppermute | solution.py:40
  126.3 1.9 %collective-permute-start.5 = (f32[1,16,64]{2,1,0:T(8,128)S(1)}, f32[1,16,64]{2,1,0:T(8,128)S(1)}, u32[]{:S(2)}, u32[]{:S(2)}) collective-permute-start(f32[1,16,64]{2,1,0:T(8,128)S(1)} %get-tuple-element.12), channel_id=1, source_target_pairs={{0,8},{2,10},{4,12},{6,14},{8,16},{10,18},{12,20},{14,22},{16,24},... | collective-permute-start | bytes 12296 | tf_op jit(solution)/shard_map/ppermute | solution.py:40
  128.3 2.6 %collective-permute-start.1 = (f32[1,2,16,256]{3,2,1,0:T(8,128)S(1)}, f32[1,2,16,256]{3,2,1,0:T(8,128)S(1)}, u32[]{:S(2)}, u32[]{:S(2)}) collective-permute-start(f32[1,2,16,256]{3,2,1,0:T(8,128)S(1)} %get-tuple-element.7), channel_id=1, source_target_pairs={{0,4},{2,6},{4,8},{6,10},{8,12},{10,14},{12,16},{14,18},{16,20},{1... | collective-permute-start | bytes 98312 | tf_op jit(solution)/shard_map/ppermute | solution.py:40
  130.9 1.9 %collective-permute-start.2 = (f32[1,2,16,256]{3,2,1,0:T(8,128)S(1)}, f32[1,2,16,256]{3,2,1,0:T(8,128)S(1)}, u32[]{:S(2)}, u32[]{:S(2)}) collective-permute-start(f32[1,2,16,256]{3,2,1,0:T(8,128)S(1)} %get-tuple-element.8), channel_id=1, source_target_pairs={{0,8},{2,10},{4,12},{6,14},{8,16},{10,18},{12,20},{14,22},{16,24},... | collective-permute-start | bytes 98312 | tf_op jit(solution)/shard_map/ppermute | solution.py:40
  132.8 1.5 %collective-permute-done.5 = f32[1,16,64]{2,1,0:T(8,128)S(1)} collective-permute-done((f32[1,16,64]{2,1,0:T(8,128)S(1)}, f32[1,16,64]{2,1,0:T(8,128)S(1)}, u32[]{:S(2)}, u32[]{:S(2)}) %collective-permute-start.5) | collective-permute-done | bytes 4128 | tf_op jit(solution)/shard_map/ppermute | solution.py:40
  134.3 0.1 copy.57
  134.5 0.8 collective-permute-done.1
  135.3 5.1 %collective-permute-done.2 = f32[1,2,16,256]{3,2,1,0:T(8,128)S(1)} collective-permute-done((f32[1,2,16,256]{3,2,1,0:T(8,128)S(1)}, f32[1,2,16,256]{3,2,1,0:T(8,128)S(1)}, u32[]{:S(2)}, u32[]{:S(2)}) %collective-permute-start.2) | collective-permute-done | bytes 32800 | tf_op jit(solution)/shard_map/ppermute | solution.py:40
  140.4 0.6 fusion.19
  (36 shorter events, 0.4 us)
Async XLA Ops:
  0.0 94.3 %copy-start = (bf16[640,1280]{1,0:T(8,128)(2,1)S(1)}, bf16[640,1280]{1,0:T(8,128)(2,1)}, u32[]{:S(2)}) copy-start(bf16[640,1280]{1,0:T(8,128)(2,1)} %param.12) | copy-start | bytes 4915204
  3.2 5.8 %copy-start.3 = (s32[1,64,64]{2,1,0:T(8,128)S(1)}, s32[1,64,64]{2,1,0:T(8,128)}, u32[]{:S(2)}) copy-start(s32[1,64,64]{2,1,0:T(8,128)} %param.15) | copy-start | bytes 49156
  3.2 37.7 %all-to-all-start = ((bf16[2,1,2,2,256,640]{5,4,3,2,1,0:T(8,128)(2,1)}), bf16[2,1,2,2,256,640]{5,4,3,2,1,0:T(8,128)(2,1)}, u32[]{:S(2)}, u32[]{:S(2)}) async-start(bf16[2,1,2,2,256,640]{5,4,3,2,1,0:T(8,128)(2,1)} %broadcast_in_dim.26), calls=%async_computation | async-start | bytes 5242880 | tf_op jit(solution)/shard_map/all_to_all | solution.py:26
  9.3 115.1 %collective-permute-start.3 = (f32[2,16,64]{2,1,0:T(8,128)S(1)}, f32[2,16,64]{2,1,0:T(8,128)S(1)}, u32[]{:S(2)}, u32[]{:S(2)}) collective-permute-start(f32[2,16,64]{2,1,0:T(8,128)S(1)} %pad_maximum_fusion.1), channel_id=1, source_target_pairs={{0,2},{2,4},{4,6},{6,8},{8,10},{10,12},{12,14},{14,16},{16,18},{18... | collective-permute-start | bytes 24584 | tf_op jit(solution)/shard_map/ppermute | solution.py:40
  50.0 2.0 %copy-start.4 = (bf16[1280,640]{1,0:T(8,128)(2,1)S(1)}, bf16[1280,640]{1,0:T(8,128)(2,1)}, u32[]{:S(2)}) copy-start(bf16[1280,640]{1,0:T(8,128)(2,1)} %param.9) | copy-start | bytes 4915204
  50.5 1.5 %copy-start.1 = (bf16[128,8,2,640]{3,1,2,0:T(8,128)(2,1)}, bf16[128,8,2,640]{3,1,2,0:T(8,128)(2,1)S(1)}, u32[]{:S(2)}) copy-start(bf16[128,8,2,640]{3,1,2,0:T(8,128)(2,1)S(1)} %copy.62) | copy-start | bytes 7864324
  73.7 5.4 %copy-start.5 = (bf16[1280,640]{1,0:T(8,128)(2,1)S(1)}, bf16[1280,640]{1,0:T(8,128)(2,1)}, u32[]{:S(2)}) copy-start(bf16[1280,640]{1,0:T(8,128)(2,1)} %param.11) | copy-start | bytes 4915204
  94.4 2.3 %copy-start.2 = (bf16[1280,64]{0,1:T(8,128)(2,1)S(1)}, bf16[1280,64]{0,1:T(8,128)(2,1)}, u32[]{:S(2)}) copy-start(bf16[1280,64]{0,1:T(8,128)(2,1)} %param.13) | copy-start | bytes 491524
  124.1 4.2 %collective-permute-start = (f32[2,2,16,256]{3,2,1,0:T(8,128)S(1)}, f32[2,2,16,256]{3,2,1,0:T(8,128)S(1)}, u32[]{:S(2)}, u32[]{:S(2)}) collective-permute-start(f32[2,2,16,256]{3,2,1,0:T(8,128)S(1)} %pad_maximum_fusion), channel_id=1, source_target_pairs={{0,2},{2,4},{4,6},{6,8},{8,10},{10,12},{12,14},{14,16},{16,18},{18... | collective-permute-start | bytes 196616 | tf_op jit(solution)/shard_map/ppermute | solution.py:40
  124.5 8.4 %collective-permute-start.4 = (f32[1,16,64]{2,1,0:T(8,128)S(1)}, f32[1,16,64]{2,1,0:T(8,128)S(1)}, u32[]{:S(2)}, u32[]{:S(2)}) collective-permute-start(f32[1,16,64]{2,1,0:T(8,128)S(1)} %get-tuple-element.11), channel_id=1, source_target_pairs={{0,4},{2,6},{4,8},{6,10},{8,12},{10,14},{12,16},{14,18},{16,20},{1... | collective-permute-start | bytes 12296 | tf_op jit(solution)/shard_map/ppermute | solution.py:40
  126.3 8.0 %collective-permute-start.5 = (f32[1,16,64]{2,1,0:T(8,128)S(1)}, f32[1,16,64]{2,1,0:T(8,128)S(1)}, u32[]{:S(2)}, u32[]{:S(2)}) collective-permute-start(f32[1,16,64]{2,1,0:T(8,128)S(1)} %get-tuple-element.12), channel_id=1, source_target_pairs={{0,8},{2,10},{4,12},{6,14},{8,16},{10,18},{12,20},{14,22},{16,24},... | collective-permute-start | bytes 12296 | tf_op jit(solution)/shard_map/ppermute | solution.py:40
  128.3 7.0 %collective-permute-start.1 = (f32[1,2,16,256]{3,2,1,0:T(8,128)S(1)}, f32[1,2,16,256]{3,2,1,0:T(8,128)S(1)}, u32[]{:S(2)}, u32[]{:S(2)}) collective-permute-start(f32[1,2,16,256]{3,2,1,0:T(8,128)S(1)} %get-tuple-element.7), channel_id=1, source_target_pairs={{0,4},{2,6},{4,8},{6,10},{8,12},{10,14},{12,16},{14,18},{16,20},{1... | collective-permute-start | bytes 98312 | tf_op jit(solution)/shard_map/ppermute | solution.py:40
  130.9 9.5 %collective-permute-start.2 = (f32[1,2,16,256]{3,2,1,0:T(8,128)S(1)}, f32[1,2,16,256]{3,2,1,0:T(8,128)S(1)}, u32[]{:S(2)}, u32[]{:S(2)}) collective-permute-start(f32[1,2,16,256]{3,2,1,0:T(8,128)S(1)} %get-tuple-element.8), channel_id=1, source_target_pairs={{0,8},{2,10},{4,12},{6,14},{8,16},{10,18},{12,20},{14,22},{16,24},... | collective-permute-start | bytes 98312 | tf_op jit(solution)/shard_map/ppermute | solution.py:40
where the time goes:
time: 142 us; the launch traced here: 141 us
  waiting for transfers between devices  38.8 us (27%)
  local copies, waits for them, and re-layouts  38.1 us (27%)
  matrix products  28.9 us (20%)
  starting transfers between devices  13.9 us (10%)
  other arithmetic  13.2 us (9%)
  blocking collectives  7.14 us (5%)
    all_to_all x1, waiting for transfers between devices, from_everyone(): lax.all_to_all(jnp.broadcast_to(x[None], (count, *x.shape)), axis, 0, 0,...  31.3 us
    ppermute x6, starting transfers between devices, shifted(): return lax.ppermute(x, axis, [(i, (i + by) % count) for i in range(count)])  8.77 us
    ppermute x6, waiting for transfers between devices, shifted(): return lax.ppermute(x, axis, [(i, (i + by) % count) for i in range(count)])  7.42 us
    all_gather x1, blocking collectives, over_pieces(): pieces = lax.all_gather(x, axis).astype(jnp.float32)  7.14 us
    dot_general x1, matrix products, shards(): jnp.dot(normed, w_key, preferred_element_type=jnp.float32)  5.55 us
    sub x1, other arithmetic, shards(): scores = scores - jnp.max(scores, axis=3, keepdims=True)  5.42 us
    dot_general x1, matrix products, shards(): jnp.einsum('shqk,skhd->sqhd', attend, value_rows, preferred_element_type=...  5.34 us
    all_to_all x1, starting transfers between devices, from_everyone(): lax.all_to_all(jnp.broadcast_to(x[None], (count, *x.shape)), axis, 0, 0,...  5.15 us
  transfers between devices with their start and end apart: 7, of which 4 were waited for; matrix products, arithmetic and copies ran while one was open for 53% of the time, Pallas kernels for 0%

commit v1 on v0

v1 whole, which is shorter than its diff:
```python
import jax
import jax.numpy as jnp
from jax import lax
from jax.experimental import pallas as pl
from jax.experimental.pallas import tpu as pltpu
from jax.sharding import PartitionSpec as P

MESH = pl.DeviceIdType.MESH
F32 = jnp.float32
BF16 = jnp.bfloat16

D = 1280
HALF = 640
TOK = 256
OUTW = 64
STRIDE = 16
WINDOW = 64
LAT = 256
FRAME = WINDOW + STRIDE
PIECES = 5
XS, ZS = 4, 8
BLK = 128
ROWS = D // ZS
SLABS = 16
OWN, OTH = 0, 1
EXP_SCALE = 1.4426950408889634 / 8.0
GUIDANCE = 3.0


def iota(shape, dim):
    return lax.broadcasted_iota(jnp.int32, shape, dim)


def kernel(
    f_ref, wq_ref, wk_ref, wv_ref, wo_ref, wh_ref, offs_ref, mask_ref, out_ref,
    wbuf, wout, whead, whz, maskv, xin, nrm, qkv, ctx, acc, rep, fold, mstage, mrecv, ostage, orecv,
    ld_sem, s_sem, fx_sem, inj_sem, a1_sem, a2_sem, b1_sem, b2_sem, sib_sem, m_sem, o_sem, oself_sem,
):
    blk = lax.axis_index("blk")
    mp = lax.axis_index("mp")
    core = lax.rem(blk, 2)
    ylo = lax.rem(blk // 2, 2)
    z = lax.rem(blk // 4, ZS)
    x = blk // (4 * ZS)

    def at(xx, zz, yy, cc):
        return ((xx * ZS + zz) * 2 + yy) * 2 + cc

    def dev(b, m):
        return (b, m)

    def ring(v, k, n):
        return lax.rem(v + k + n, n)

    side = dev(at(x, z, 1 - ylo, core), mp)
    cross = dev(at(x, z, 1 - ylo, core), 1 - mp)
    xdev = [dev(at(ring(x, k, XS), z, ylo, core), mp) for k in (1, 2, 3)]
    zplus = dev(at(x, ring(z, 1, ZS), ylo, core), mp)
    zminus = dev(at(x, ring(z, -1, ZS), ylo, core), mp)
    sibling = dev(at(x, z, ylo, 1 - core), mp)
    window = blk + 2 - 4 * ylo

    def window_of(b):
        return b + 2 - 4 * lax.rem(b // 2, 2)

    loads = []

    def load(src, dst):
        copy = pltpu.make_async_copy(src, dst, ld_sem.at[len(loads)])
        copy.start()
        loads.append(copy)
        return copy

    ld_wo = load(wo_ref, wout)
    ld_wh = load(wh_ref, whead)
    ld_mask = load(mask_ref.at[0], maskv)
    ld_w = []
    for m, ref in enumerate((wq_ref, wk_ref, wv_ref)):
        for j in range(5):
            ld_w.append(load(ref.at[:, pl.ds(128 * j, 128)], wbuf.at[OWN, 5 * m + j]))

    barrier = pltpu.get_barrier_semaphore()

    def greet(d):
        pl.semaphore_signal(barrier, inc=1, device_id=d, device_id_type=MESH)

    for d in [side, cross, *xdev, zplus, zminus, sibling]:
        greet(d)
    for j in range(1, PIECES):
        greet(dev(ring(blk, j, BLK), mp))
        greet(dev(ring(blk, -j, BLK), mp))
    for j in range(PIECES):
        target = ring(window, j, BLK)
        source = window_of(ring(blk, -j, BLK))
        greet(dev(target, 1 - mp))
        greet(dev(source, 1 - mp))
        if j != 2:
            greet(dev(target, mp))
            greet(dev(source, mp))

    @pl.when(ylo == 0)
    def _():
        greet(dev(ring(window, 2, BLK), mp))
        greet(dev(window_of(ring(blk, -2, BLK)), mp))

    shift = offs_ref[0] - STRIDE * blk
    ld_wh.wait()
    lane = iota((1, 128), 1)
    low = lane < 64
    twice = jnp.concatenate([whead[...], whead[...]], axis=1)
    whz[...] = jnp.where(low, twice.astype(F32), 0.0).astype(BF16)
    ld_wo.wait()
    for r in range(0, HALF, 128):
        prod = jnp.dot(wout[r : r + 128, :], twice, preferred_element_type=F32)
        head = prod.astype(BF16).astype(F32)
        wbuf[OWN, 15, r : r + 128, :] = jnp.where(low, head, prod - head).astype(BF16)
        wbuf[OWN, 15, HALF + r : HALF + r + 128, :] = jnp.zeros((128, 128), BF16)

    ld_mask.wait()
    widen = (iota((WINDOW, LAT), 0) == (iota((WINDOW, LAT), 1) >> 2)).astype(F32).astype(BF16)
    wide = jnp.dot(maskv[...].astype(F32).astype(BF16), widen, preferred_element_type=F32)
    move = (iota((FRAME, WINDOW), 0) - iota((FRAME, WINDOW), 1) == shift).astype(F32).astype(BF16)
    mstage[...] = jnp.dot(move, wide.astype(BF16), preferred_element_type=F32)
    mrecv[0] = mstage[0:STRIDE, :]

    for copy in ld_w:
        copy.wait()
    pl.semaphore_wait(barrier, 34 + 2 * (1 - ylo))

    sends = []

    def remote(src, dst, sem, d):
        copy = pltpu.make_async_remote_copy(
            src_ref=src, dst_ref=dst, send_sem=s_sem.at[len(sends)], recv_sem=sem,
            device_id=d, device_id_type=MESH,
        )
        sends.append(copy)
        return copy

    def send(src, dst, sem, d):
        remote(src, dst, sem, d).start()

    def arrived(dst, sem, d):
        pltpu.make_async_remote_copy(
            src_ref=dst, dst_ref=dst, send_sem=s_sem.at[0], recv_sem=sem,
            device_id=d, device_id_type=MESH,
        ).wait_recv()

    base_a = core * 8
    slab_a = base_a + x
    slab_b = base_a + 4 + x

    def rows(zz, part=None):
        if part is None:
            return pl.ds(pl.multiple_of(zz * ROWS, 16), ROWS)
        return pl.ds(pl.multiple_of(zz * ROWS + part * (ROWS // 2), 16), ROWS // 2)

    def piece_a(which):
        return wbuf.at[which, slab_a, rows(z), :]

    def piece_b(which, zz, part=None):
        return wbuf.at[which, slab_b, rows(zz, part), :]

    def bundle(zz, part):
        return wbuf.at[OTH, pl.ds(base_a + 2 * part, 2), rows(zz), :]

    def bundle_whole(zz):
        return wbuf.at[OTH, pl.ds(base_a, 4), rows(zz), :]

    send(piece_b(OWN, z), piece_b(OTH, z), inj_sem.at[1], cross)
    send(piece_a(OWN), piece_a(OTH), inj_sem.at[0], cross)
    half = pl.ds(pl.multiple_of(HALF * mp, 128), HALF)
    other_half = pl.ds(pl.multiple_of(HALF * (1 - mp), 128), HALF)
    for p in range(2):
        dst = xin.at[p, :, half]
        send(f_ref.at[0, mp, p], dst, fx_sem.at[0, p], side)
        send(f_ref.at[0, 1 - mp, p], dst, fx_sem.at[1, p], cross)
    for j in range(1, PIECES):
        send(mstage.at[pl.ds(STRIDE * j, STRIDE)], mrecv.at[j], m_sem, dev(ring(blk, j, BLK), mp))

    def forward_x(ref):
        for k in range(3):
            send(ref, ref, b2_sem.at[k], xdev[k])

    arrived(piece_b(OTH, z), inj_sem.at[1], cross)
    send(piece_b(OTH, z), piece_b(OTH, z), b1_sem.at[0, 0], zplus)
    send(piece_b(OTH, z), piece_b(OTH, z), b1_sem.at[1, 0], zminus)
    arrived(piece_a(OTH), inj_sem.at[0], cross)
    for k in range(3):
        send(piece_a(OTH), piece_a(OTH), a1_sem.at[k], xdev[k])
    forward_x(piece_b(OTH, z))

    def b1_step(step):
        behind, ahead = ring(z, -step, ZS), ring(z, step, ZS)
        if step < 4:
            for direction, zz, d in ((0, behind, zplus), (1, ahead, zminus)):
                ref = piece_b(OTH, zz)
                arrived(ref, b1_sem.at[direction, step - 1], d)
                if step < 3:
                    send(ref, ref, b1_sem.at[direction, step], d)
                else:
                    part = piece_b(OTH, zz, direction)
                    send(part, part, b1_sem.at[direction, step], d)
                forward_x(ref)
        else:
            for direction in range(2):
                ref = piece_b(OTH, behind, direction)
                arrived(ref, b1_sem.at[direction, 3], zplus)
                forward_x(ref)
            whole = wbuf.at[OTH, slab_b]
            send(whole, whole, sib_sem, sibling)

    def a2_start():
        for k in range(3):
            ref = wbuf.at[OTH, base_a + ring(x, -(k + 1), XS), rows(z), :]
            arrived(ref, a1_sem.at[k], xdev[k])
        for part in range(2):
            for direction, d in ((0, zplus), (1, zminus)):
                ref = bundle(z, part)
                send(ref, ref, a2_sem.at[direction, 0, part], d)
        send(bundle_whole(z), bundle_whole(z), sib_sem, sibling)

    def a2_step(step):
        behind, ahead = ring(z, -step, ZS), ring(z, step, ZS)
        if step < 4:
            for part in range(2):
                for direction, zz, d in ((0, behind, zplus), (1, ahead, zminus)):
                    ref = bundle(zz, part)
                    arrived(ref, a2_sem.at[direction, step - 1, part], d)
                    if step < 3 or part == direction:
                        send(ref, ref, a2_sem.at[direction, step, part], d)
            for zz in (behind, ahead):
                send(bundle_whole(zz), bundle_whole(zz), sib_sem, sibling)
        else:
            for direction in range(2):
                arrived(bundle(behind, direction), a2_sem.at[direction, 3, direction], zplus)
            send(bundle_whole(behind), bundle_whole(behind), sib_sem, sibling)

    def b2_finish():
        for k in range(3):
            ref = wbuf.at[OTH, base_a + 4 + ring(x, -(k + 1), XS)]
            arrived(ref, b2_sem.at[k], xdev[k])
            send(ref, ref, sib_sem, sibling)

    def sibling_finish():
        ref = wbuf.at[OTH, pl.ds((1 - core) * 8, 8)]
        arrived(ref, sib_sem, sibling)

    def norm(p):
        def body(i, carry):
            r = pl.ds(pl.multiple_of(i * 64, 64), 64)
            rows_f = xin[p, r, :].astype(F32)
            mean = jnp.mean(rows_f, axis=1, keepdims=True)
            centred = rows_f - mean
            var = jnp.mean(centred * centred, axis=1, keepdims=True)
            nrm[p, r, :] = (centred * lax.rsqrt(var + 1e-05)).astype(BF16)
            return carry

        lax.fori_loop(0, 4, body, 0)
        acc[p] = jnp.dot(xin[p], whz[...], preferred_element_type=F32)

    def project(p, which):
        def body(i, carry):
            w = jnp.concatenate([wbuf[which, 2 * i], wbuf[which, 2 * i + 1]], axis=1)
            r = jnp.dot(nrm[p], w, preferred_element_type=F32)
            qkv[:, pl.ds(pl.multiple_of(256 * i, 256), 256)] = r.astype(BF16)
            return carry

        lax.fori_loop(0, 7, body, 0)
        r = jnp.dot(nrm[p], wbuf[which, 14], preferred_element_type=F32)
        qkv[:, 1792:1920] = r.astype(BF16)

    def attend(p, which):
        def body(i, carry):
            def part(first):
                return qkv[:, pl.ds(pl.multiple_of(first + 128 * i, 128), 128)]

            q, k, v = part(0), part(HALF), part(2 * HALF)
            vo = jnp.concatenate([v, jnp.ones((TOK, 128), BF16)], axis=1)
            outs = []
            for e in range(2):
                keep = low if e == 0 else jnp.logical_not(low)
                qm = jnp.where(keep, q.astype(F32), 0.0).astype(BF16)
                s = lax.dot_general(qm, k, (((1,), (1,)), ((), ())), preferred_element_type=F32)
                s = s - jnp.max(s, axis=1, keepdims=True)
                ex = jnp.exp2(s * EXP_SCALE).astype(BF16)
                o = jnp.dot(ex, vo, preferred_element_type=F32)
                outs.append(o[:, :128] / o[:, 128:])
            joined = jnp.where(low, outs[0], outs[1]).astype(BF16)
            ctx[:, pl.ds(pl.multiple_of(128 * i, 128), 128)] = joined
            return carry

        lax.fori_loop(0, 5, body, 0)
        acc[p] += jnp.dot(ctx[...], wbuf[which, 15, 0:HALF, :], preferred_element_type=F32)

    def selections(r, carry):
        f = iota((FRAME, TOK), 0) - shift
        t = iota((FRAME, TOK), 1) - 16 * r
        hit = (f >= 4 * t) & (f < 4 * t + 4) & (t >= 0) & (t < 16)
        rep[pl.ds(pl.multiple_of(r * FRAME, 16), FRAME), :] = hit.astype(F32).astype(BF16)
        hit = iota((256, LAT), 1) == 16 * r + (iota((256, LAT), 0) & 15)
        fold[r] = hit.astype(F32).astype(BF16)
        return carry

    b1_step(1)
    a2_start()
    b1_step(2)
    lax.fori_loop(0, 8, selections, 0)
    b1_step(3)
    lax.fori_loop(8, 16, selections, 0)
    b1_step(4)
    a2_step(1)
    for h, part in ((0, half), (1, other_half)):
        arrived(xin.at[0, :, part], fx_sem.at[h, 0], side if h == 0 else cross)
    norm(0)
    project(0, OWN)
    a2_step(2)
    attend(0, OWN)
    a2_step(3)
    for h, part in ((0, half), (1, other_half)):
        arrived(xin.at[1, :, part], fx_sem.at[h, 1], side if h == 0 else cross)
    norm(1)
    a2_step(4)
    b2_finish()
    project(1, OWN)
    attend(1, OWN)
    sibling_finish()
    for p in range(2):
        project(p, OTH)
        attend(p, OTH)

    guided = acc[0] + GUIDANCE * (acc[1] - acc[0])
    high = guided.astype(BF16)
    rest = (guided - high.astype(F32)).astype(BF16)
    both = jnp.concatenate([high, rest], axis=1)
    column = ((iota((FRAME, 256), 0) - shift) & 3) == ((iota((FRAME, 256), 1) >> 4) & 3)
    total = jnp.zeros((FRAME, LAT), F32)
    for r in range(16):
        y = jnp.dot(rep[r * FRAME : (r + 1) * FRAME, :], both, preferred_element_type=F32)
        y = jnp.where(column, y, 0.0).astype(BF16)
        total = total + jnp.dot(y, fold[r], preferred_element_type=F32)
    ostage[...] = total

    conditional = None
    for j in range(PIECES):
        src = ostage.at[pl.ds(STRIDE * j, STRIDE)]
        dst = orecv.at[mp, j]
        target = ring(window, j, BLK)
        send(src, dst, o_sem.at[0], dev(target, 1 - mp))
        if j != 2:
            send(src, dst, o_sem.at[1], dev(target, mp))
        else:
            conditional = remote(src, dst, oself_sem, dev(target, mp))

    @pl.when(ylo == 0)
    def _():
        conditional.start()

    @pl.when(ylo == 1)
    def _():
        orecv[mp, 2] = ostage[2 * STRIDE : 3 * STRIDE, :]

    arrived(mrecv.at[pl.ds(1, 4)], m_sem, sibling)
    arrived(orecv.at[mp, pl.ds(0, 4)], o_sem.at[1], sibling)
    arrived(orecv.at[1 - mp], o_sem.at[0], sibling)

    @pl.when(ylo == 0)
    def _():
        arrived(orecv.at[mp, 2], oself_sem, sibling)

    weight = mrecv[0]
    for j in range(1, PIECES):
        weight = weight + mrecv[j]
    for b in range(2):
        value = orecv[b, 0] * mrecv[0]
        for j in range(1, PIECES):
            value = value + orecv[b, j] * mrecv[j]
        out_ref[b] = value / weight

    for copy in sends:
        if copy is conditional:
            @pl.when(ylo == 0)
            def _():
                conditional.wait_send()
        else:
            copy.wait_send()


def shards(features, w_query, w_key, w_value, w_out, w_head, offsets, blend_mask):
    anyspace = pl.BlockSpec(memory_space=pl.ANY)
    return pl.pallas_call(
        kernel,
        out_shape=jax.ShapeDtypeStruct((2, STRIDE, LAT), F32),
        in_specs=[anyspace] * 6 + [pl.BlockSpec(memory_space=pltpu.SMEM), anyspace],
        out_specs=pl.BlockSpec(memory_space=pltpu.VMEM),
        scratch_shapes=[
            pltpu.VMEM((2, SLABS, D, 128), BF16),
            pltpu.VMEM((HALF, D), BF16),
            pltpu.VMEM((D, OUTW), BF16),
            pltpu.VMEM((D, 128), BF16),
            pltpu.VMEM((WINDOW, WINDOW), jnp.int32),
            pltpu.VMEM((2, TOK, D), BF16),
            pltpu.VMEM((2, TOK, D), BF16),
            pltpu.VMEM((TOK, 3 * HALF), BF16),
            pltpu.VMEM((TOK, HALF), BF16),
            pltpu.VMEM((2, TOK, 128), F32),
            pltpu.VMEM((16 * FRAME, TOK), BF16),
            pltpu.VMEM((16, 256, LAT), BF16),
            pltpu.VMEM((FRAME, LAT), F32),
            pltpu.VMEM((PIECES, STRIDE, LAT), F32),
            pltpu.VMEM((FRAME, LAT), F32),
            pltpu.VMEM((2, PIECES, STRIDE, LAT), F32),
            pltpu.SemaphoreType.DMA((20,)),
            pltpu.SemaphoreType.DMA((110,)),
            pltpu.SemaphoreType.DMA((2, 2)),
            pltpu.SemaphoreType.DMA((2,)),
            pltpu.SemaphoreType.DMA((3,)),
            pltpu.SemaphoreType.DMA((2, 4, 2)),
            pltpu.SemaphoreType.DMA((2, 4)),
            pltpu.SemaphoreType.DMA((3,)),
            pltpu.SemaphoreType.DMA,
            pltpu.SemaphoreType.DMA,
            pltpu.SemaphoreType.DMA((2,)),
            pltpu.SemaphoreType.DMA,
        ],
        compiler_params=pltpu.CompilerParams(
            collective_id=0, has_side_effects=True, vmem_limit_bytes=60 * 1024 * 1024
        ),
    )(features, w_query, w_key, w_value, w_out, w_head, offsets, blend_mask)


def solution(mesh):
    return jax.shard_map(
        shards,
        mesh=mesh,
        in_specs=(
            P("blk", None, None, None, "mp"),
            P(None, "mp"),
            P(None, "mp"),
            P(None, "mp"),
            P("mp", None),
            P(),
            P("blk"),
            P("blk", None, None),
        ),
        out_specs=P(None, "blk", None),
        check_vma=False,
    )
```

time: 142 us -> 70.9 us (0.50)
  the two profiles are of different devices: /device:TPU:8 before, /device:TPU:1 now
where the time goes in v1:
time: 70.9 us; the launch traced here: 70.8 us
  Pallas kernels  66.9 us (94%)
  local copies, waits for them, and re-layouts  3.18 us (4%)
    pallas_call x1, Pallas kernels, shards(): pl.pallas_call(kernel, out_shape=jax.ShapeDtypeStruct((2, STRIDE, LAT), F...  66.9 us
    unnamed x2, local copies, waits for them, and re-layouts  3.18 us

profile of v1, /device:TPU:1, one launch (start us, length us, event | category | flops | bytes accessed | tf_op | source)
XLA Modules:
  0.0 70.8 jit_solution(4331736123971256132)
XLA Ops:
  0.7 1.8 %copy.9.wh_ref = bf16[1280,64]{1,0:T(8,128)(2,1)} copy(bf16[1280,64]{0,1:T(8,128)(2,1)} %param.13) | data formatting | bytes 327680 | tf_op args[5]
  2.5 66.9 %shard_map.82 = f32[2,16,256]{2,1,0:T(8,128)} custom-call(bf16[1,2,2,256,640]{4,3,2,1,0:T(8,128)(2,1)} %f_ref.1, bf16[1280,640]{1,0:T(8,128)(2,1)} %wq_ref.1, bf16[1280,640]{1,0:T(8,128)(2,1)} %wk_ref.1, bf16[1280,640]{1,0:T(8,128)(2,1)} %wv_ref.1, bf16[640,1280]{1,0:T(8,128)(2,1)} %wo_ref.1, bf16[1280,64]{1,0:T(8,128)(2,1)} %copy.9.wh_ref, ...), custom_call_target="tpu_custom_call" | custom-call | tf_op jit(solution)/shard_map/pallas_call | solution.py:391
  69.4 1.4 %copy.12 = f32[2,16,256]{2,1,0:T(8,128)} copy(f32[2,16,256]{2,1,0:T(8,128)} %shard_map.82) | data formatting | bytes 65536

commit v2 on v1

--- a/solution.py
+++ b/solution.py
@@ -27,13 +27,17 @@
 GUIDANCE = 3.0
 
 
+def dot_t(a, b):
+    return lax.dot_general(a, b, (((1,), (1,)), ((), ())), preferred_element_type=F32)
+
+
 def iota(shape, dim):
     return lax.broadcasted_iota(jnp.int32, shape, dim)
 
 
 def kernel(
     f_ref, wq_ref, wk_ref, wv_ref, wo_ref, wh_ref, offs_ref, mask_ref, out_ref,
-    wbuf, wout, whead, whz, maskv, xin, nrm, qkv, ctx, acc, rep, fold, mstage, mrecv, ostage, orecv,
+    wbuf, wout, whead, twice, maskv, xin, nrm, qkv, ctx, acc, rep, fold, mstage, mrecv, ostage, orecv,
     ld_sem, s_sem, fx_sem, inj_sem, a1_sem, a2_sem, b1_sem, b2_sem, sib_sem, m_sem, o_sem, oself_sem,
 ):
     blk = lax.axis_index("blk")
@@ -60,9 +64,6 @@
     sibling = dev(at(x, z, ylo, 1 - core), mp)
     window = blk + 2 - 4 * ylo
 
-    def window_of(b):
-        return b + 2 - 4 * lax.rem(b // 2, 2)
-
     loads = []
 
     def load(src, dst):
@@ -86,32 +87,16 @@
 
     for d in [side, cross, *xdev, zplus, zminus, sibling]:
         greet(d)
-    for j in range(1, PIECES):
-        greet(dev(ring(blk, j, BLK), mp))
-        greet(dev(ring(blk, -j, BLK), mp))
-    for j in range(PIECES):
-        target = ring(window, j, BLK)
-        source = window_of(ring(blk, -j, BLK))
-        greet(dev(target, 1 - mp))
-        greet(dev(source, 1 - mp))
-        if j != 2:
-            greet(dev(target, mp))
-            greet(dev(source, mp))
-
-    @pl.when(ylo == 0)
-    def _():
-        greet(dev(ring(window, 2, BLK), mp))
-        greet(dev(window_of(ring(blk, -2, BLK)), mp))
 
     shift = offs_ref[0] - STRIDE * blk
     ld_wh.wait()
     lane = iota((1, 128), 1)
     low = lane < 64
-    twice = jnp.concatenate([whead[...], whead[...]], axis=1)
-    whz[...] = jnp.where(low, twice.astype(F32), 0.0).astype(BF16)
+    twice[0:OUTW, :] = whead[...]
+    twice[OUTW:, :] = whead[...]
     ld_wo.wait()
     for r in range(0, HALF, 128):
-        prod = jnp.dot(wout[r : r + 128, :], twice, preferred_element_type=F32)
+        prod = dot_t(wout[r : r + 128, :], twice[...])
         head = prod.astype(BF16).astype(F32)
         wbuf[OWN, 15, r : r + 128, :] = jnp.where(low, head, prod - head).astype(BF16)
         wbuf[OWN, 15, HALF + r : HALF + r + 128, :] = jnp.zeros((128, 128), BF16)
@@ -125,7 +110,7 @@
 
     for copy in ld_w:
         copy.wait()
-    pl.semaphore_wait(barrier, 34 + 2 * (1 - ylo))
+    pl.semaphore_wait(barrier, 8)
 
     sends = []
 
@@ -161,8 +146,8 @@
     def piece_b(which, zz, part=None):
         return wbuf.at[which, slab_b, rows(zz, part), :]
 
-    def bundle(zz, part):
-        return wbuf.at[OTH, pl.ds(base_a + 2 * part, 2), rows(zz), :]
+    def slab_piece(k, zz):
+        return wbuf.at[OTH, base_a + ring(x, -k, XS), rows(zz), :]
 
     def bundle_whole(zz):
         return wbuf.at[OTH, pl.ds(base_a, 4), rows(zz), :]
@@ -175,8 +160,6 @@
         dst = xin.at[p, :, half]
         send(f_ref.at[0, mp, p], dst, fx_sem.at[0, p], side)
         send(f_ref.at[0, 1 - mp, p], dst, fx_sem.at[1, p], cross)
-    for j in range(1, PIECES):
-        send(mstage.at[pl.ds(STRIDE * j, STRIDE)], mrecv.at[j], m_sem, dev(ring(blk, j, BLK), mp))
 
     def forward_x(ref):
         for k in range(3):
@@ -188,6 +171,8 @@
     arrived(piece_a(OTH), inj_sem.at[0], cross)
     for k in range(3):
         send(piece_a(OTH), piece_a(OTH), a1_sem.at[k], xdev[k])
+    for direction, d in ((0, zplus), (1, zminus)):
+        send(piece_a(OTH), piece_a(OTH), a2_sem.at[direction, 0, 0], d)
     forward_x(piece_b(OTH, z))
 
     def b1_step(step):
@@ -211,30 +196,27 @@
             send(whole, whole, sib_sem, sibling)
 
     def a2_start():
-        for k in range(3):
-            ref = wbuf.at[OTH, base_a + ring(x, -(k + 1), XS), rows(z), :]
-            arrived(ref, a1_sem.at[k], xdev[k])
-        for part in range(2):
+        for k in (1, 3, 2):
+            ref = slab_piece(k, z)
+            arrived(ref, a1_sem.at[k - 1], xdev[k - 1])
             for direction, d in ((0, zplus), (1, zminus)):
-                ref = bundle(z, part)
-                send(ref, ref, a2_sem.at[direction, 0, part], d)
+                send(ref, ref, a2_sem.at[direction, 0, k], d)
         send(bundle_whole(z), bundle_whole(z), sib_sem, sibling)
 
-    def a2_step(step):
+    def a2_step(step, ks):
         behind, ahead = ring(z, -step, ZS), ring(z, step, ZS)
-        if step < 4:
-            for part in range(2):
-                for direction, zz, d in ((0, behind, zplus), (1, ahead, zminus)):
-                    ref = bundle(zz, part)
-                    arrived(ref, a2_sem.at[direction, step - 1, part], d)
-                    if step < 3 or part == direction:
-                        send(ref, ref, a2_sem.at[direction, step, part], d)
-            for zz in (behind, ahead):
+        for k in ks:
+            for direction, zz, d in ((0, behind, zplus), (1, ahead, zminus)):
+                last = (k < 2) == (direction == 0)
+                if step == 4 and not last:
+                    continue
+                ref = slab_piece(k, zz)
+                arrived(ref, a2_sem.at[direction, step - 1, k], d)
+                if step < 3 or (step == 3 and last):
+                    send(ref, ref, a2_sem.at[direction, step, k], d)
+        if ks[-1] != 0:
+            for zz in (behind, ahead) if step < 4 else (behind,):
                 send(bundle_whole(zz), bundle_whole(zz), sib_sem, sibling)
-        else:
-            for direction in range(2):
-                arrived(bundle(behind, direction), a2_sem.at[direction, 3, direction], zplus)
-            send(bundle_whole(behind), bundle_whole(behind), sib_sem, sibling)
 
     def b2_finish():
         for k in range(3):
@@ -257,41 +239,41 @@
             return carry
 
         lax.fori_loop(0, 4, body, 0)
-        acc[p] = jnp.dot(xin[p], whz[...], preferred_element_type=F32)
-
-    def project(p, which):
-        def body(i, carry):
-            w = jnp.concatenate([wbuf[which, 2 * i], wbuf[which, 2 * i + 1]], axis=1)
+        acc[p] = jnp.where(low, dot_t(xin[p], twice[...]), 0.0)
+
+    lane3 = iota((1, 256), 1)
+
+    def project(p, which, first, last):
+        for i in range(first, last):
+            if i < 7:
+                w = jnp.concatenate([wbuf[which, 2 * i], wbuf[which, 2 * i + 1]], axis=1)
+            else:
+                w = wbuf[which, 14]
             r = jnp.dot(nrm[p], w, preferred_element_type=F32)
-            qkv[:, pl.ds(pl.multiple_of(256 * i, 256), 256)] = r.astype(BF16)
-            return carry
-
-        lax.fori_loop(0, 7, body, 0)
-        r = jnp.dot(nrm[p], wbuf[which, 14], preferred_element_type=F32)
-        qkv[:, 1792:1920] = r.astype(BF16)
-
-    def attend(p, which):
-        def body(i, carry):
-            def part(first):
-                return qkv[:, pl.ds(pl.multiple_of(first + 128 * i, 128), 128)]
-
-            q, k, v = part(0), part(HALF), part(2 * HALF)
+            if i < 2:
+                r = r * EXP_SCALE
+            elif i == 2:
+                r = r * jnp.where(lane3 < 128, EXP_SCALE, 1.0)
+            qkv[:, 256 * i : 256 * i + r.shape[1]] = r.astype(BF16)
+
+    def attend(p, which, first, last):
+        for i in range(first, last):
+            q = qkv[:, 128 * i : 128 * i + 128]
+            k = qkv[:, HALF + 128 * i : HALF + 128 * i + 128]
+            v = qkv[:, 2 * HALF + 128 * i : 2 * HALF + 128 * i + 128]
             vo = jnp.concatenate([v, jnp.ones((TOK, 128), BF16)], axis=1)
             outs = []
             for e in range(2):
                 keep = low if e == 0 else jnp.logical_not(low)
-                qm = jnp.where(keep, q.astype(F32), 0.0).astype(BF16)
-                s = lax.dot_general(qm, k, (((1,), (1,)), ((), ())), preferred_element_type=F32)
+                qm = q * keep.astype(F32).astype(BF16)
+                s = dot_t(qm, k)
                 s = s - jnp.max(s, axis=1, keepdims=True)
-                ex = jnp.exp2(s * EXP_SCALE).astype(BF16)
-                o = jnp.dot(ex, vo, preferred_element_type=F32)
-                outs.append(o[:, :128] / o[:, 128:])
-            joined = jnp.where(low, outs[0], outs[1]).astype(BF16)
-            ctx[:, pl.ds(pl.multiple_of(128 * i, 128), 128)] = joined
-            return carry
-
-        lax.fori_loop(0, 5, body, 0)
-        acc[p] += jnp.dot(ctx[...], wbuf[which, 15, 0:HALF, :], preferred_element_type=F32)
+                outs.append(jnp.dot(jnp.exp2(s).astype(BF16), vo, preferred_element_type=F32))
+            top = jnp.where(low, outs[0][:, :128], outs[1][:, :128])
+            bottom = jnp.where(low, outs[0][:, 128:], outs[1][:, 128:])
+            ctx[:, 128 * i : 128 * i + 128] = (top / bottom).astype(BF16)
+        if last == 5:
+            acc[p] += jnp.dot(ctx[...], wbuf[which, 15, 0:HALF, :], preferred_element_type=F32)
 
     def selections(r, carry):
         f = iota((FRAME, TOK), 0) - shift
@@ -302,32 +284,41 @@
         fold[r] = hit.astype(F32).astype(BF16)
         return carry
 
+    def features_of(p):
+        for h, part in ((0, half), (1, other_half)):
+            arrived(xin.at[p, :, part], fx_sem.at[h, p], side if h == 0 else cross)
+
+    rest = (1, 3, 2)
     b1_step(1)
+    a2_step(1, (0,))
     a2_start()
+    lax.fori_loop(0, 8, selections, 0)
     b1_step(2)
-    lax.fori_loop(0, 8, selections, 0)
+    a2_step(2, (0,))
+    lax.fori_loop(8, 16, selections, 0)
+    a2_step(1, rest)
     b1_step(3)
-    lax.fori_loop(8, 16, selections, 0)
+    features_of(0)
+    norm(0)
+    a2_step(3, (0,))
+    a2_step(2, rest)
     b1_step(4)
-    a2_step(1)
-    for h, part in ((0, half), (1, other_half)):
-        arrived(xin.at[0, :, part], fx_sem.at[h, 0], side if h == 0 else cross)
-    norm(0)
-    project(0, OWN)
-    a2_step(2)
-    attend(0, OWN)
-    a2_step(3)
-    for h, part in ((0, half), (1, other_half)):
-        arrived(xin.at[1, :, part], fx_sem.at[h, 1], side if h == 0 else cross)
+    project(0, OWN, 0, 8)
+    a2_step(3, rest)
+    attend(0, OWN, 0, 5)
+    features_of(1)
     norm(1)
-    a2_step(4)
+    a2_step(4, (0,) + rest)
+    project(1, OWN, 0, 8)
     b2_finish()
-    project(1, OWN)
-    attend(1, OWN)
+    attend(1, OWN, 0, 5)
     sibling_finish()
     for p in range(2):
-        project(p, OTH)
-        attend(p, OTH)
+        project(p, OTH, 0, 8)
+        attend(p, OTH, 0, 5)
+
+    for j in range(1, PIECES):
+        send(mstage.at[pl.ds(STRIDE * j, STRIDE)], mrecv.at[j], m_sem, dev(ring(blk, j, BLK), mp))
 
     guided = acc[0] + GUIDANCE * (acc[1] - acc[0])
     high = guided.astype(BF16)
@@ -396,8 +387,8 @@
         scratch_shapes=[
             pltpu.VMEM((2, SLABS, D, 128), BF16),
             pltpu.VMEM((HALF, D), BF16),
-            pltpu.VMEM((D, OUTW), BF16),
-            pltpu.VMEM((D, 128), BF16),
+            pltpu.VMEM((OUTW, D), BF16),
+            pltpu.VMEM((128, D), BF16),
             pltpu.VMEM((WINDOW, WINDOW), jnp.int32),
             pltpu.VMEM((2, TOK, D), BF16),
             pltpu.VMEM((2, TOK, D), BF16),
@@ -415,7 +406,7 @@
             pltpu.SemaphoreType.DMA((2, 2)),
             pltpu.SemaphoreType.DMA((2,)),
             pltpu.SemaphoreType.DMA((3,)),
-            pltpu.SemaphoreType.DMA((2, 4, 2)),
+            pltpu.SemaphoreType.DMA((2, 4, 4)),
             pltpu.SemaphoreType.DMA((2, 4)),
             pltpu.SemaphoreType.DMA((3,)),
             pltpu.SemaphoreType.DMA,
@@ -426,7 +417,7 @@
         compiler_params=pltpu.CompilerParams(
             collective_id=0, has_side_effects=True, vmem_limit_bytes=60 * 1024 * 1024
         ),
-    )(features, w_query, w_key, w_value, w_out, w_head, offsets, blend_mask)
+    )(features, w_query, w_key, w_value, w_out, w_head.T, offsets, blend_mask)
 
 
 def solution(mesh):

time: 70.9 us -> 56.3 us (0.79)
  Pallas kernels: 66.9 us -> 54.1 us
  local copies, waits for them, and re-layouts: 3.18 us -> 1.38 us
    pallas_call x1, Pallas kernels: 66.9 us -> 54.1 us  [shards(): pl.pallas_call(kernel, out_shape=jax.ShapeDtypeStruct((2, STRIDE, LAT), F...]
    unnamed x2 -> x1, local copies, waits for them, and re-layouts: 3.18 us -> 1.38 us
where the time goes in v2:
time: 56.3 us; the launch traced here: 56.1 us
  Pallas kernels  54.1 us (96%)
  local copies, waits for them, and re-layouts  1.38 us (2%)
  between operations  0.66 us (1%)
    pallas_call x1, Pallas kernels, shards(): pl.pallas_call(kernel, out_shape=jax.ShapeDtypeStruct((2, STRIDE, LAT), F...  54.1 us
    unnamed x1, local copies, waits for them, and re-layouts  1.38 us

profile of v2, /device:TPU:1, one launch (start us, length us, event | category | flops | bytes accessed | tf_op | source)
XLA Modules:
  0.0 56.1 jit_solution(11403819940552251618)
XLA Ops:
  0.7 54.1 %shard_map.82 = f32[2,16,256]{2,1,0:T(8,128)} custom-call(bf16[1,2,2,256,640]{4,3,2,1,0:T(8,128)(2,1)} %f_ref.1, bf16[1280,640]{1,0:T(8,128)(2,1)} %wq_ref.1, bf16[1280,640]{1,0:T(8,128)(2,1)} %wk_ref.1, bf16[1280,640]{1,0:T(8,128)(2,1)} %wv_ref.1, bf16[640,1280]{1,0:T(8,128)(2,1)} %wo_ref.1, bf16[64,1280]{1,0:T(8,128)(2,1)} %bitcast.1, ...), custom_call_target="tpu_custom_call" | custom-call | tf_op jit(solution)/shard_map/pallas_call | solution.py:382
  54.8 1.4 %copy.11 = f32[2,16,256]{2,1,0:T(8,128)} copy(f32[2,16,256]{2,1,0:T(8,128)} %shard_map.82) | data formatting | bytes 65536

commit v3 on v2

--- a/solution.py
+++ b/solution.py
@@ -23,6 +23,11 @@
 ROWS = D // ZS
 SLABS = 16
 OWN, OTH = 0, 1
+SLAB = ((0, 2), (2, 2), (1, 3), (0, 4), (0, 0), (1, 0), (2, 0), (0, 1), (1, 2), (0, 3), (2, 3), (1, 4), (1, 1), (2, 1), (2, 4))
+FIRST_TILES = ((4, 5), (6, 7), (12, 13), (14,))
+LAST_TILES = ((0, 8), (1, 9), (2, 10), (3, 11))
+CHUNKS = 2
+CROWS = TOK // CHUNKS
 EXP_SCALE = 1.4426950408889634 / 8.0
 GUIDANCE = 3.0
 
@@ -64,6 +69,14 @@
     sibling = dev(at(x, z, ylo, 1 - core), mp)
     window = blk + 2 - 4 * ylo
 
+    barrier = pltpu.get_barrier_semaphore()
+
+    def greet(d):
+        pl.semaphore_signal(barrier, inc=1, device_id=d, device_id_type=MESH)
+
+    for d in [side, cross, *xdev, zplus, zminus, sibling]:
+        greet(d)
+
     loads = []
 
     def load(src, dst):
@@ -76,17 +89,9 @@
     ld_wh = load(wh_ref, whead)
     ld_mask = load(mask_ref.at[0], maskv)
     ld_w = []
-    for m, ref in enumerate((wq_ref, wk_ref, wv_ref)):
-        for j in range(5):
-            ld_w.append(load(ref.at[:, pl.ds(128 * j, 128)], wbuf.at[OWN, 5 * m + j]))
-
-    barrier = pltpu.get_barrier_semaphore()
-
-    def greet(d):
-        pl.semaphore_signal(barrier, inc=1, device_id=d, device_id_type=MESH)
-
-    for d in [side, cross, *xdev, zplus, zminus, sibling]:
-        greet(d)
+    for i, (m, j) in enumerate(SLAB):
+        ref = (wq_ref, wk_ref, wv_ref)[m]
+        ld_w.append(load(ref.at[:, pl.ds(128 * j, 128)], wbuf.at[OWN, i]))
 
     shift = offs_ref[0] - STRIDE * blk
     ld_wh.wait()
@@ -149,17 +154,16 @@
     def slab_piece(k, zz):
         return wbuf.at[OTH, base_a + ring(x, -k, XS), rows(zz), :]
 
-    def bundle_whole(zz):
-        return wbuf.at[OTH, pl.ds(base_a, 4), rows(zz), :]
-
     send(piece_b(OWN, z), piece_b(OTH, z), inj_sem.at[1], cross)
     send(piece_a(OWN), piece_a(OTH), inj_sem.at[0], cross)
     half = pl.ds(pl.multiple_of(HALF * mp, 128), HALF)
     other_half = pl.ds(pl.multiple_of(HALF * (1 - mp), 128), HALF)
     for p in range(2):
-        dst = xin.at[p, :, half]
-        send(f_ref.at[0, mp, p], dst, fx_sem.at[0, p], side)
-        send(f_ref.at[0, 1 - mp, p], dst, fx_sem.at[1, p], cross)
+        for i in range(CHUNKS):
+            part = pl.ds(CROWS * i, CROWS)
+            dst = xin.at[p, part, half]
+            send(f_ref.at[0, mp, p, part], dst, fx_sem.at[0, p, i], side)
+            send(f_ref.at[0, 1 - mp, p, part], dst, fx_sem.at[1, p, i], cross)
 
     def forward_x(ref):
         for k in range(3):
@@ -174,6 +178,7 @@
     for direction, d in ((0, zplus), (1, zminus)):
         send(piece_a(OTH), piece_a(OTH), a2_sem.at[direction, 0, 0], d)
     forward_x(piece_b(OTH, z))
+    send(piece_a(OTH), piece_a(OTH), sib_sem.at[0], sibling)
 
     def b1_step(step):
         behind, ahead = ring(z, -step, ZS), ring(z, step, ZS)
@@ -193,7 +198,7 @@
                 arrived(ref, b1_sem.at[direction, 3], zplus)
                 forward_x(ref)
             whole = wbuf.at[OTH, slab_b]
-            send(whole, whole, sib_sem, sibling)
+            send(whole, whole, sib_sem.at[1], sibling)
 
     def a2_start():
         for k in (1, 3, 2):
@@ -201,7 +206,7 @@
             arrived(ref, a1_sem.at[k - 1], xdev[k - 1])
             for direction, d in ((0, zplus), (1, zminus)):
                 send(ref, ref, a2_sem.at[direction, 0, k], d)
-        send(bundle_whole(z), bundle_whole(z), sib_sem, sibling)
+            send(ref, ref, sib_sem.at[0], sibling)
 
     def a2_step(step, ks):
         behind, ahead = ring(z, -step, ZS), ring(z, step, ZS)
@@ -214,53 +219,41 @@
                 arrived(ref, a2_sem.at[direction, step - 1, k], d)
                 if step < 3 or (step == 3 and last):
                     send(ref, ref, a2_sem.at[direction, step, k], d)
-        if ks[-1] != 0:
-            for zz in (behind, ahead) if step < 4 else (behind,):
-                send(bundle_whole(zz), bundle_whole(zz), sib_sem, sibling)
+                send(ref, ref, sib_sem.at[0], sibling)
 
     def b2_finish():
         for k in range(3):
             ref = wbuf.at[OTH, base_a + 4 + ring(x, -(k + 1), XS)]
             arrived(ref, b2_sem.at[k], xdev[k])
-            send(ref, ref, sib_sem, sibling)
-
-    def sibling_finish():
-        ref = wbuf.at[OTH, pl.ds((1 - core) * 8, 8)]
-        arrived(ref, sib_sem, sibling)
-
-    def norm(p):
-        def body(i, carry):
-            r = pl.ds(pl.multiple_of(i * 64, 64), 64)
-            rows_f = xin[p, r, :].astype(F32)
+            send(ref, ref, sib_sem.at[1], sibling)
+
+    def norm(p, i):
+        for r in range(CROWS * i, CROWS * (i + 1), 32):
+            rows_f = xin[p, r : r + 32, :].astype(F32)
             mean = jnp.mean(rows_f, axis=1, keepdims=True)
             centred = rows_f - mean
             var = jnp.mean(centred * centred, axis=1, keepdims=True)
-            nrm[p, r, :] = (centred * lax.rsqrt(var + 1e-05)).astype(BF16)
-            return carry
-
-        lax.fori_loop(0, 4, body, 0)
-        acc[p] = jnp.where(low, dot_t(xin[p], twice[...]), 0.0)
-
-    lane3 = iota((1, 256), 1)
-
-    def project(p, which, first, last):
-        for i in range(first, last):
-            if i < 7:
-                w = jnp.concatenate([wbuf[which, 2 * i], wbuf[which, 2 * i + 1]], axis=1)
-            else:
-                w = wbuf[which, 14]
-            r = jnp.dot(nrm[p], w, preferred_element_type=F32)
-            if i < 2:
-                r = r * EXP_SCALE
-            elif i == 2:
-                r = r * jnp.where(lane3 < 128, EXP_SCALE, 1.0)
-            qkv[:, 256 * i : 256 * i + r.shape[1]] = r.astype(BF16)
-
-    def attend(p, which, first, last):
-        for i in range(first, last):
-            q = qkv[:, 128 * i : 128 * i + 128]
-            k = qkv[:, HALF + 128 * i : HALF + 128 * i + 128]
-            v = qkv[:, 2 * HALF + 128 * i : 2 * HALF + 128 * i + 128]
+            nrm[p, r : r + 32, :] = (centred * lax.rsqrt(var + 1e-05)).astype(BF16)
+        r = CROWS * i
+        acc[p, r : r + CROWS, :] = jnp.where(low, dot_t(xin[p, r : r + CROWS, :], twice[...]), 0.0)
+
+    def project(p, which, tiles, i=None):
+        first, count = (0, TOK) if i is None else (CROWS * i, CROWS)
+        for tile in tiles:
+            parts = [wbuf[which, t] for t in tile]
+            w = jnp.concatenate(parts, axis=1) if len(parts) > 1 else parts[0]
+            r = jnp.dot(nrm[p, first : first + count, :], w, preferred_element_type=F32)
+            for n, t in enumerate(tile):
+                m, j = SLAB[t]
+                part = r[:, 128 * n : 128 * n + 128]
+                if m == 0:
+                    part = part * EXP_SCALE
+                at_col = 384 * j + 128 * m
+                qkv[p, first : first + count, at_col : at_col + 128] = part.astype(BF16)
+
+    def attend(p, which, pairs):
+        for i in pairs:
+            q, k, v = (qkv[p, :, 384 * i + 128 * m : 384 * i + 128 * m + 128] for m in range(3))
             vo = jnp.concatenate([v, jnp.ones((TOK, 128), BF16)], axis=1)
             outs = []
             for e in range(2):
@@ -271,22 +264,30 @@
                 outs.append(jnp.dot(jnp.exp2(s).astype(BF16), vo, preferred_element_type=F32))
             top = jnp.where(low, outs[0][:, :128], outs[1][:, :128])
             bottom = jnp.where(low, outs[0][:, 128:], outs[1][:, 128:])
-            ctx[:, 128 * i : 128 * i + 128] = (top / bottom).astype(BF16)
-        if last == 5:
-            acc[p] += jnp.dot(ctx[...], wbuf[which, 15, 0:HALF, :], preferred_element_type=F32)
-
-    def selections(r, carry):
+            ctx[p, :, 128 * i : 128 * i + 128] = (top / bottom).astype(BF16)
+
+    def join(p, which):
+        acc[p] += jnp.dot(ctx[p], wbuf[which, 15, 0:HALF, :], preferred_element_type=F32)
+
+    def selections(n, carry):
         f = iota((FRAME, TOK), 0) - shift
-        t = iota((FRAME, TOK), 1) - 16 * r
-        hit = (f >= 4 * t) & (f < 4 * t + 4) & (t >= 0) & (t < 16)
-        rep[pl.ds(pl.multiple_of(r * FRAME, 16), FRAME), :] = hit.astype(F32).astype(BF16)
-        hit = iota((256, LAT), 1) == 16 * r + (iota((256, LAT), 0) & 15)
-        fold[r] = hit.astype(F32).astype(BF16)
+        for r in (2 * n, 2 * n + 1):
+            t = iota((FRAME, TOK), 1) - 16 * r
+            hit = (f >= 4 * t) & (f < 4 * t + 4) & (t >= 0) & (t < 16)
+            rep[pl.ds(pl.multiple_of(r * FRAME, 16), FRAME), :] = hit.astype(F32).astype(BF16)
+        lanes = iota((256, LAT), 0)
+        hit = iota((256, LAT), 1) == 32 * n + 16 * (lanes >> 7) + (lanes & 15)
+        fold[n] = hit.astype(F32).astype(BF16)
         return carry
 
-    def features_of(p):
+    def features_of(p, i):
         for h, part in ((0, half), (1, other_half)):
-            arrived(xin.at[p, :, part], fx_sem.at[h, p], side if h == 0 else cross)
+            arrived(xin.at[p, pl.ds(CROWS * i, CROWS), part], fx_sem.at[h, p, i], side if h == 0 else cross)
+
+    def own_chunk(p, i):
+        features_of(p, i)
+        norm(p, i)
+        project(p, OWN, FIRST_TILES + LAST_TILES, i)
 
     rest = (1, 3, 2)
     b1_step(1)
@@ -295,41 +296,51 @@
     lax.fori_loop(0, 8, selections, 0)
     b1_step(2)
     a2_step(2, (0,))
-    lax.fori_loop(8, 16, selections, 0)
     a2_step(1, rest)
+    own_chunk(0, 0)
     b1_step(3)
-    features_of(0)
-    norm(0)
     a2_step(3, (0,))
+    own_chunk(0, 1)
     a2_step(2, rest)
     b1_step(4)
-    project(0, OWN, 0, 8)
+    attend(0, OWN, (0, 1, 2, 3, 4))
+    join(0, OWN)
+    own_chunk(1, 0)
     a2_step(3, rest)
-    attend(0, OWN, 0, 5)
-    features_of(1)
-    norm(1)
+    own_chunk(1, 1)
+    b2_finish()
+    attend(1, OWN, (0, 1, 2))
     a2_step(4, (0,) + rest)
-    project(1, OWN, 0, 8)
-    b2_finish()
-    attend(1, OWN, 0, 5)
-    sibling_finish()
+    attend(1, OWN, (3, 4))
+    join(1, OWN)
+    arrived(wbuf.at[OTH, pl.ds((1 - core) * 8 + 4, 4)], sib_sem.at[1], sibling)
     for p in range(2):
-        project(p, OTH, 0, 8)
-        attend(p, OTH, 0, 5)
+        project(p, OTH, FIRST_TILES)
+    for p in range(2):
+        attend(p, OTH, (0, 1))
+    arrived(wbuf.at[OTH, pl.ds((1 - core) * 8, 4)], sib_sem.at[0], sibling)
+    for p in range(2):
+        project(p, OTH, LAST_TILES)
+    for p in range(2):
+        attend(p, OTH, (2, 3, 4))
+        join(p, OTH)
 
     for j in range(1, PIECES):
         send(mstage.at[pl.ds(STRIDE * j, STRIDE)], mrecv.at[j], m_sem, dev(ring(blk, j, BLK), mp))
 
     guided = acc[0] + GUIDANCE * (acc[1] - acc[0])
-    high = guided.astype(BF16)
-    rest = (guided - high.astype(F32)).astype(BF16)
-    both = jnp.concatenate([high, rest], axis=1)
+    guided = guided + pltpu.roll(guided, 64, 1)
+    high = guided.astype(BF16).astype(F32)
+    both = jnp.where(low, high, guided - high).astype(BF16)
     column = ((iota((FRAME, 256), 0) - shift) & 3) == ((iota((FRAME, 256), 1) >> 4) & 3)
     total = jnp.zeros((FRAME, LAT), F32)
-    for r in range(16):
-        y = jnp.dot(rep[r * FRAME : (r + 1) * FRAME, :], both, preferred_element_type=F32)
-        y = jnp.where(column, y, 0.0).astype(BF16)
-        total = total + jnp.dot(y, fold[r], preferred_element_type=F32)
+    for n in range(8):
+        y = [
+            jnp.dot(rep[r * FRAME : (r + 1) * FRAME, :], both, preferred_element_type=F32)
+            for r in (2 * n, 2 * n + 1)
+        ]
+        y = jnp.where(column, jnp.concatenate(y, axis=1), 0.0).astype(BF16)
+        total = total + jnp.dot(y, fold[n], preferred_element_type=F32)
     ostage[...] = total
 
     conditional = None
@@ -392,24 +403,24 @@
             pltpu.VMEM((WINDOW, WINDOW), jnp.int32),
             pltpu.VMEM((2, TOK, D), BF16),
             pltpu.VMEM((2, TOK, D), BF16),
-            pltpu.VMEM((TOK, 3 * HALF), BF16),
-            pltpu.VMEM((TOK, HALF), BF16),
+            pltpu.VMEM((2, TOK, 3 * HALF), BF16),
+            pltpu.VMEM((2, TOK, HALF), BF16),
             pltpu.VMEM((2, TOK, 128), F32),
             pltpu.VMEM((16 * FRAME, TOK), BF16),
-            pltpu.VMEM((16, 256, LAT), BF16),
+            pltpu.VMEM((8, 256, LAT), BF16),
             pltpu.VMEM((FRAME, LAT), F32),
             pltpu.VMEM((PIECES, STRIDE, LAT), F32),
             pltpu.VMEM((FRAME, LAT), F32),
             pltpu.VMEM((2, PIECES, STRIDE, LAT), F32),
             pltpu.SemaphoreType.DMA((20,)),
-            pltpu.SemaphoreType.DMA((110,)),
-            pltpu.SemaphoreType.DMA((2, 2)),
+            pltpu.SemaphoreType.DMA((140,)),
+            pltpu.SemaphoreType.DMA((2, 2, CHUNKS)),
             pltpu.SemaphoreType.DMA((2,)),
             pltpu.SemaphoreType.DMA((3,)),
             pltpu.SemaphoreType.DMA((2, 4, 4)),
             pltpu.SemaphoreType.DMA((2, 4)),
             pltpu.SemaphoreType.DMA((3,)),
-            pltpu.SemaphoreType.DMA,
+            pltpu.SemaphoreType.DMA((2,)),
             pltpu.SemaphoreType.DMA,
             pltpu.SemaphoreType.DMA((2,)),
             pltpu.SemaphoreType.DMA,

time: 56.3 us -> 53.8 us (0.956)
  Pallas kernels: 54.1 us -> 51.6 us
    pallas_call x1, Pallas kernels: 54.1 us -> 51.6 us  [shards(): pl.pallas_call(kernel, out_shape=jax.ShapeDtypeStruct((2, STRIDE, LAT), F...]
where the time goes in v3:
time: 53.8 us; the launch traced here: 53.7 us
  Pallas kernels  51.6 us (96%)
  local copies, waits for them, and re-layouts  1.38 us (3%)
  between operations  0.66 us (1%)
    pallas_call x1, Pallas kernels, shards(): pl.pallas_call(kernel, out_shape=jax.ShapeDtypeStruct((2, STRIDE, LAT), F...  51.6 us
    unnamed x1, local copies, waits for them, and re-layouts  1.38 us

profile of v3, /device:TPU:1, one launch (start us, length us, event | category | flops | bytes accessed | tf_op | source)
XLA Modules:
  0.0 53.7 jit_solution(5282956803824654984)
XLA Ops:
  0.7 51.6 %shard_map.82 = f32[2,16,256]{2,1,0:T(8,128)} custom-call(bf16[1,2,2,256,640]{4,3,2,1,0:T(8,128)(2,1)} %f_ref.1, bf16[1280,640]{1,0:T(8,128)(2,1)} %wq_ref.1, bf16[1280,640]{1,0:T(8,128)(2,1)} %wk_ref.1, bf16[1280,640]{1,0:T(8,128)(2,1)} %wv_ref.1, bf16[640,1280]{1,0:T(8,128)(2,1)} %wo_ref.1, bf16[64,1280]{1,0:T(8,128)(2,1)} %bitcast.1, ...), custom_call_target="tpu_custom_call" | custom-call | tf_op jit(solution)/shard_map/pallas_call | solution.py:393
  52.3 1.4 %copy.11 = f32[2,16,256]{2,1,0:T(8,128)} copy(f32[2,16,256]{2,1,0:T(8,128)} %shard_map.82) | data formatting | bytes 65536

commit v4 on v3

--- a/solution.py
+++ b/solution.py
@@ -20,12 +20,14 @@
 PIECES = 5
 XS, ZS = 4, 8
 BLK = 128
-ROWS = D // ZS
+ZP = 4
+ROWS = D // ZP
+LAST = ZP // 2
 SLABS = 16
 OWN, OTH = 0, 1
 SLAB = ((0, 2), (2, 2), (1, 3), (0, 4), (0, 0), (1, 0), (2, 0), (0, 1), (1, 2), (0, 3), (2, 3), (1, 4), (1, 1), (2, 1), (2, 4))
-FIRST_TILES = ((4, 5), (6, 7), (12, 13), (14,))
-LAST_TILES = ((0, 8), (1, 9), (2, 10), (3, 11))
+TILES_B = ((4, 5), (6, 7), (12, 13), (14,))
+TILES_A = ((0, 8), (1, 9), (2, 10), (3, 11))
 CHUNKS = 2
 CROWS = TOK // CHUNKS
 EXP_SCALE = 1.4426950408889634 / 8.0
@@ -71,6 +73,8 @@
 
     barrier = pltpu.get_barrier_semaphore()
 
+    low = iota((1, 128), 1) < 64
+
     def greet(d):
         pl.semaphore_signal(barrier, inc=1, device_id=d, device_id_type=MESH)
 
@@ -93,10 +97,77 @@
         ref = (wq_ref, wk_ref, wv_ref)[m]
         ld_w.append(load(ref.at[:, pl.ds(128 * j, 128)], wbuf.at[OWN, i]))
 
-    shift = offs_ref[0] - STRIDE * blk
+    pl.semaphore_wait(barrier, 8)
+
+    sends = []
+
+    def remote(src, dst, sem, d):
+        copy = pltpu.make_async_remote_copy(
+            src_ref=src, dst_ref=dst, send_sem=s_sem.at[len(sends)], recv_sem=sem,
+            device_id=d, device_id_type=MESH,
+        )
+        sends.append(copy)
+        return copy
+
+    def send(src, dst, sem, d):
+        remote(src, dst, sem, d).start()
+
+    def arrived(dst, sem, d):
+        pltpu.make_async_remote_copy(
+            src_ref=dst, dst_ref=dst, send_sem=s_sem.at[0], recv_sem=sem,
+            device_id=d, device_id_type=MESH,
+        ).wait_recv()
+
+    base_a = core * 8
+    zp = lax.rem(z, ZP)
+    slab_a = base_a + x
+    slab_b = base_a + 4 + x
+
+    def rows(zz, part=None):
+        if part is None:
+            return pl.ds(pl.multiple_of(zz * ROWS, 16), ROWS)
+        return pl.ds(pl.multiple_of(zz * ROWS + part * (ROWS // 2), 16), ROWS // 2)
+
+    def piece_a(which):
+        return wbuf.at[which, slab_a, rows(zp), :]
+
+    def piece_b(which, zz, part=None):
+        return wbuf.at[which, slab_b, rows(zz, part), :]
+
+    def slab_piece(k, zz):
+        return wbuf.at[OTH, base_a + ring(x, -k, XS), rows(zz), :]
+
+    def inject(n, sem, i):
+        if i < 15:
+            m, j = SLAB[i]
+            src = (wq_ref, wk_ref, wv_ref)[m].at[rows(zp), pl.ds(128 * j, 128)]
+        else:
+            src = wbuf.at[OWN, 15, rows(zp), :]
+
+        @pl.when((core == i // 8) & (x == i % 4))
+        def _():
+            pltpu.make_async_remote_copy(
+                src_ref=src, dst_ref=wbuf.at[OTH, i, rows(zp), :], send_sem=s_sem.at[n], recv_sem=sem,
+                device_id=cross, device_id_type=MESH,
+            ).start()
+
+    remote(piece_a(OTH), piece_a(OTH), inj_sem.at[0], cross)
+    remote(piece_b(OTH, zp), piece_b(OTH, zp), inj_sem.at[1], cross)
+    for i in (0, 1, 2, 3, 8, 9, 10, 11):
+        inject(0, inj_sem.at[0], i)
+    for i in (4, 5, 6, 7, 12, 13, 14):
+        inject(1, inj_sem.at[1], i)
+    half = pl.ds(pl.multiple_of(HALF * mp, 128), HALF)
+    other_half = pl.ds(pl.multiple_of(HALF * (1 - mp), 128), HALF)
+
+    def send_features(p, i):
+        part = pl.ds(CROWS * i, CROWS)
+        dst = xin.at[p, part, half]
+        send(f_ref.at[0, mp, p, part], dst, fx_sem.at[0, p, i], side)
+        send(f_ref.at[0, 1 - mp, p, part], dst, fx_sem.at[1, p, i], cross)
+
+    send_features(0, 0)
     ld_wh.wait()
-    lane = iota((1, 128), 1)
-    low = lane < 64
     twice[0:OUTW, :] = whead[...]
     twice[OUTW:, :] = whead[...]
     ld_wo.wait()
@@ -106,6 +177,12 @@
         wbuf[OWN, 15, r : r + 128, :] = jnp.where(low, head, prod - head).astype(BF16)
         wbuf[OWN, 15, HALF + r : HALF + r + 128, :] = jnp.zeros((128, 128), BF16)
 
+    inject(1, inj_sem.at[1], 15)
+    send_features(0, 1)
+    for i in range(CHUNKS):
+        send_features(1, i)
+
+    shift = offs_ref[0] - STRIDE * blk
     ld_mask.wait()
     widen = (iota((WINDOW, LAT), 0) == (iota((WINDOW, LAT), 1) >> 2)).astype(F32).astype(BF16)
     wide = jnp.dot(maskv[...].astype(F32).astype(BF16), widen, preferred_element_type=F32)
@@ -113,80 +190,29 @@
     mstage[...] = jnp.dot(move, wide.astype(BF16), preferred_element_type=F32)
     mrecv[0] = mstage[0:STRIDE, :]
 
-    for copy in ld_w:
-        copy.wait()
-    pl.semaphore_wait(barrier, 8)
-
-    sends = []
-
-    def remote(src, dst, sem, d):
-        copy = pltpu.make_async_remote_copy(
-            src_ref=src, dst_ref=dst, send_sem=s_sem.at[len(sends)], recv_sem=sem,
-            device_id=d, device_id_type=MESH,
-        )
-        sends.append(copy)
-        return copy
-
-    def send(src, dst, sem, d):
-        remote(src, dst, sem, d).start()
-
-    def arrived(dst, sem, d):
-        pltpu.make_async_remote_copy(
-            src_ref=dst, dst_ref=dst, send_sem=s_sem.at[0], recv_sem=sem,
-            device_id=d, device_id_type=MESH,
-        ).wait_recv()
-
-    base_a = core * 8
-    slab_a = base_a + x
-    slab_b = base_a + 4 + x
-
-    def rows(zz, part=None):
-        if part is None:
-            return pl.ds(pl.multiple_of(zz * ROWS, 16), ROWS)
-        return pl.ds(pl.multiple_of(zz * ROWS + part * (ROWS // 2), 16), ROWS // 2)
-
-    def piece_a(which):
-        return wbuf.at[which, slab_a, rows(z), :]
-
-    def piece_b(which, zz, part=None):
-        return wbuf.at[which, slab_b, rows(zz, part), :]
-
-    def slab_piece(k, zz):
-        return wbuf.at[OTH, base_a + ring(x, -k, XS), rows(zz), :]
-
-    send(piece_b(OWN, z), piece_b(OTH, z), inj_sem.at[1], cross)
-    send(piece_a(OWN), piece_a(OTH), inj_sem.at[0], cross)
-    half = pl.ds(pl.multiple_of(HALF * mp, 128), HALF)
-    other_half = pl.ds(pl.multiple_of(HALF * (1 - mp), 128), HALF)
-    for p in range(2):
-        for i in range(CHUNKS):
-            part = pl.ds(CROWS * i, CROWS)
-            dst = xin.at[p, part, half]
-            send(f_ref.at[0, mp, p, part], dst, fx_sem.at[0, p, i], side)
-            send(f_ref.at[0, 1 - mp, p, part], dst, fx_sem.at[1, p, i], cross)
 
     def forward_x(ref):
         for k in range(3):
             send(ref, ref, b2_sem.at[k], xdev[k])
 
-    arrived(piece_b(OTH, z), inj_sem.at[1], cross)
-    send(piece_b(OTH, z), piece_b(OTH, z), b1_sem.at[0, 0], zplus)
-    send(piece_b(OTH, z), piece_b(OTH, z), b1_sem.at[1, 0], zminus)
     arrived(piece_a(OTH), inj_sem.at[0], cross)
     for k in range(3):
         send(piece_a(OTH), piece_a(OTH), a1_sem.at[k], xdev[k])
     for direction, d in ((0, zplus), (1, zminus)):
         send(piece_a(OTH), piece_a(OTH), a2_sem.at[direction, 0, 0], d)
-    forward_x(piece_b(OTH, z))
+    arrived(piece_b(OTH, zp), inj_sem.at[1], cross)
+    send(piece_b(OTH, zp), piece_b(OTH, zp), b1_sem.at[0, 0], zplus)
+    send(piece_b(OTH, zp), piece_b(OTH, zp), b1_sem.at[1, 0], zminus)
+    forward_x(piece_b(OTH, zp))
     send(piece_a(OTH), piece_a(OTH), sib_sem.at[0], sibling)
 
     def b1_step(step):
-        behind, ahead = ring(z, -step, ZS), ring(z, step, ZS)
-        if step < 4:
+        behind, ahead = ring(zp, -step, ZP), ring(zp, step, ZP)
+        if step < LAST:
             for direction, zz, d in ((0, behind, zplus), (1, ahead, zminus)):
                 ref = piece_b(OTH, zz)
                 arrived(ref, b1_sem.at[direction, step - 1], d)
-                if step < 3:
+                if step < LAST - 1:
                     send(ref, ref, b1_sem.at[direction, step], d)
                 else:
                     part = piece_b(OTH, zz, direction)
@@ -195,29 +221,29 @@
         else:
             for direction in range(2):
                 ref = piece_b(OTH, behind, direction)
-                arrived(ref, b1_sem.at[direction, 3], zplus)
+                arrived(ref, b1_sem.at[direction, LAST - 1], zplus)
                 forward_x(ref)
             whole = wbuf.at[OTH, slab_b]
             send(whole, whole, sib_sem.at[1], sibling)
 
     def a2_start():
         for k in (1, 3, 2):
-            ref = slab_piece(k, z)
+            ref = slab_piece(k, zp)
             arrived(ref, a1_sem.at[k - 1], xdev[k - 1])
             for direction, d in ((0, zplus), (1, zminus)):
                 send(ref, ref, a2_sem.at[direction, 0, k], d)
             send(ref, ref, sib_sem.at[0], sibling)
 
     def a2_step(step, ks):
-        behind, ahead = ring(z, -step, ZS), ring(z, step, ZS)
+        behind, ahead = ring(zp, -step, ZP), ring(zp, step, ZP)
         for k in ks:
             for direction, zz, d in ((0, behind, zplus), (1, ahead, zminus)):
                 last = (k < 2) == (direction == 0)
-                if step == 4 and not last:
+                if step == LAST and not last:
                     continue
                 ref = slab_piece(k, zz)
                 arrived(ref, a2_sem.at[direction, step - 1, k], d)
-                if step < 3 or (step == 3 and last):
+                if step < LAST - 1 or (step == LAST - 1 and last):
                     send(ref, ref, a2_sem.at[direction, step, k], d)
                 send(ref, ref, sib_sem.at[0], sibling)
 
@@ -287,42 +313,40 @@
     def own_chunk(p, i):
         features_of(p, i)
         norm(p, i)
-        project(p, OWN, FIRST_TILES + LAST_TILES, i)
-
-    rest = (1, 3, 2)
-    b1_step(1)
+        project(p, OWN, TILES_B + TILES_A, i)
+
     a2_step(1, (0,))
     a2_start()
+    b1_step(1)
     lax.fori_loop(0, 8, selections, 0)
+    for copy in ld_w:
+        copy.wait()
+    own_chunk(0, 0)
+    a2_step(1, (1, 3))
+    own_chunk(0, 1)
+    a2_step(1, (2,))
     b1_step(2)
+    attend(0, OWN, (0, 1, 2))
     a2_step(2, (0,))
-    a2_step(1, rest)
-    own_chunk(0, 0)
-    b1_step(3)
-    a2_step(3, (0,))
-    own_chunk(0, 1)
-    a2_step(2, rest)
-    b1_step(4)
-    attend(0, OWN, (0, 1, 2, 3, 4))
+    attend(0, OWN, (3, 4))
     join(0, OWN)
     own_chunk(1, 0)
-    a2_step(3, rest)
+    a2_step(2, (1, 3, 2))
     own_chunk(1, 1)
+    attend(1, OWN, (0, 1))
     b2_finish()
-    attend(1, OWN, (0, 1, 2))
-    a2_step(4, (0,) + rest)
-    attend(1, OWN, (3, 4))
+    attend(1, OWN, (2, 3, 4))
     join(1, OWN)
+    arrived(wbuf.at[OTH, pl.ds((1 - core) * 8, 4)], sib_sem.at[0], sibling)
+    for p in range(2):
+        project(p, OTH, TILES_A)
+    for p in range(2):
+        attend(p, OTH, (2, 3))
     arrived(wbuf.at[OTH, pl.ds((1 - core) * 8 + 4, 4)], sib_sem.at[1], sibling)
     for p in range(2):
-        project(p, OTH, FIRST_TILES)
+        project(p, OTH, TILES_B)
     for p in range(2):
-        attend(p, OTH, (0, 1))
-    arrived(wbuf.at[OTH, pl.ds((1 - core) * 8, 4)], sib_sem.at[0], sibling)
-    for p in range(2):
-        project(p, OTH, LAST_TILES)
-    for p in range(2):
-        attend(p, OTH, (2, 3, 4))
+        attend(p, OTH, (0, 1, 4))
         join(p, OTH)
 
     for j in range(1, PIECES):

time: 53.8 us -> 51.3 us (0.954)
  Pallas kernels: 51.6 us -> 49.1 us
    pallas_call x1, Pallas kernels: 51.6 us -> 49.1 us  [shards(): pl.pallas_call(kernel, out_shape=jax.ShapeDtypeStruct((2, STRIDE, LAT), F...]
where the time goes in v4:
time: 51.3 us; the launch traced here: 51.2 us
  Pallas kernels  49.1 us (96%)
  local copies, waits for them, and re-layouts  1.38 us (3%)
  between operations  0.66 us (1%)
    pallas_call x1, Pallas kernels, shards(): pl.pallas_call(kernel, out_shape=jax.ShapeDtypeStruct((2, STRIDE, LAT), F...  49.1 us
    unnamed x1, local copies, waits for them, and re-layouts  1.38 us

profile of v4, /device:TPU:1, one launch (start us, length us, event | category | flops | bytes accessed | tf_op | source)
XLA Modules:
  0.0 51.2 jit_solution(11575750189056933801)
XLA Ops:
  0.7 49.1 %shard_map.82 = f32[2,16,256]{2,1,0:T(8,128)} custom-call(bf16[1,2,2,256,640]{4,3,2,1,0:T(8,128)(2,1)} %f_ref.1, bf16[1280,640]{1,0:T(8,128)(2,1)} %wq_ref.1, bf16[1280,640]{1,0:T(8,128)(2,1)} %wk_ref.1, bf16[1280,640]{1,0:T(8,128)(2,1)} %wv_ref.1, bf16[640,1280]{1,0:T(8,128)(2,1)} %wo_ref.1, bf16[64,1280]{1,0:T(8,128)(2,1)} %bitcast.1, ...), custom_call_target="tpu_custom_call" | custom-call | tf_op jit(solution)/shard_map/pallas_call | solution.py:417
  49.8 1.4 %copy.11 = f32[2,16,256]{2,1,0:T(8,128)} copy(f32[2,16,256]{2,1,0:T(8,128)} %shard_map.82) | data formatting | bytes 65536

commit v5 on v4

--- a/solution.py
+++ b/solution.py
@@ -191,9 +191,9 @@
     mrecv[0] = mstage[0:STRIDE, :]
 
 
-    def forward_x(ref):
-        for k in range(3):
-            send(ref, ref, b2_sem.at[k], xdev[k])
+    def forward_x(ref, last=0):
+        for k in (1, 0, 2):
+            send(ref, ref, b2_sem.at[k, last], xdev[k])
 
     arrived(piece_a(OTH), inj_sem.at[0], cross)
     for k in range(3):
@@ -205,6 +205,7 @@
     send(piece_b(OTH, zp), piece_b(OTH, zp), b1_sem.at[1, 0], zminus)
     forward_x(piece_b(OTH, zp))
     send(piece_a(OTH), piece_a(OTH), sib_sem.at[0], sibling)
+    send(piece_b(OTH, zp), piece_b(OTH, zp), sib_sem.at[1], sibling)
 
     def b1_step(step):
         behind, ahead = ring(zp, -step, ZP), ring(zp, step, ZP)
@@ -218,13 +219,13 @@
                     part = piece_b(OTH, zz, direction)
                     send(part, part, b1_sem.at[direction, step], d)
                 forward_x(ref)
+                send(ref, ref, sib_sem.at[1], sibling)
         else:
             for direction in range(2):
                 ref = piece_b(OTH, behind, direction)
                 arrived(ref, b1_sem.at[direction, LAST - 1], zplus)
-                forward_x(ref)
-            whole = wbuf.at[OTH, slab_b]
-            send(whole, whole, sib_sem.at[1], sibling)
+                forward_x(ref, 1)
+            send(piece_b(OTH, behind), piece_b(OTH, behind), sib_sem.at[1], sibling)
 
     def a2_start():
         for k in (1, 3, 2):
@@ -247,10 +248,21 @@
                     send(ref, ref, a2_sem.at[direction, step, k], d)
                 send(ref, ref, sib_sem.at[0], sibling)
 
-    def b2_finish():
+    def b2_slab(k, zz):
+        return wbuf.at[OTH, base_a + 4 + ring(x, -(k + 1), XS), rows(zz), :]
+
+    def b2_first():
         for k in range(3):
-            ref = wbuf.at[OTH, base_a + 4 + ring(x, -(k + 1), XS)]
-            arrived(ref, b2_sem.at[k], xdev[k])
+            near = [b2_slab(k, ring(zp, n, ZP)) for n in (0, 1, 3)]
+            whole = wbuf.at[OTH, base_a + 4 + ring(x, -(k + 1), XS), pl.ds(0, 3 * ROWS), :]
+            arrived(whole, b2_sem.at[k, 0], xdev[k])
+            for ref in near:
+                send(ref, ref, sib_sem.at[1], sibling)
+
+    def b2_last():
+        for k in (0, 2, 1):
+            ref = b2_slab(k, ring(zp, 2, ZP))
+            arrived(ref, b2_sem.at[k, 1], xdev[k])
             send(ref, ref, sib_sem.at[1], sibling)
 
     def norm(p, i):
@@ -332,11 +344,11 @@
     join(0, OWN)
     own_chunk(1, 0)
     a2_step(2, (1, 3, 2))
+    b2_first()
     own_chunk(1, 1)
-    attend(1, OWN, (0, 1))
-    b2_finish()
-    attend(1, OWN, (2, 3, 4))
+    attend(1, OWN, (0, 1, 2, 3, 4))
     join(1, OWN)
+    b2_last()
     arrived(wbuf.at[OTH, pl.ds((1 - core) * 8, 4)], sib_sem.at[0], sibling)
     for p in range(2):
         project(p, OTH, TILES_A)
@@ -443,7 +455,7 @@
             pltpu.SemaphoreType.DMA((3,)),
             pltpu.SemaphoreType.DMA((2, 4, 4)),
             pltpu.SemaphoreType.DMA((2, 4)),
-            pltpu.SemaphoreType.DMA((3,)),
+            pltpu.SemaphoreType.DMA((3, 2)),
             pltpu.SemaphoreType.DMA((2,)),
             pltpu.SemaphoreType.DMA,
             pltpu.SemaphoreType.DMA((2,)),

time: 51.3 us -> 50.9 us (level)
  no operation moved by 1% of the time
where the time goes in v5:
time: 50.9 us; the launch traced here: 50.8 us
  Pallas kernels  48.7 us (96%)
  local copies, waits for them, and re-layouts  1.38 us (3%)
  between operations  0.66 us (1%)
    pallas_call x1, Pallas kernels, shards(): pl.pallas_call(kernel, out_shape=jax.ShapeDtypeStruct((2, STRIDE, LAT), F...  48.7 us
    unnamed x1, local copies, waits for them, and re-layouts  1.38 us

profile of v5, /device:TPU:1, one launch (start us, length us, event | category | flops | bytes accessed | tf_op | source)
XLA Modules:
  0.0 50.8 jit_solution(1669223354943702340)
XLA Ops:
  0.7 48.7 %shard_map.82 = f32[2,16,256]{2,1,0:T(8,128)} custom-call(bf16[1,2,2,256,640]{4,3,2,1,0:T(8,128)(2,1)} %f_ref.1, bf16[1280,640]{1,0:T(8,128)(2,1)} %wq_ref.1, bf16[1280,640]{1,0:T(8,128)(2,1)} %wk_ref.1, bf16[1280,640]{1,0:T(8,128)(2,1)} %wv_ref.1, bf16[640,1280]{1,0:T(8,128)(2,1)} %wo_ref.1, bf16[64,1280]{1,0:T(8,128)(2,1)} %bitcast.1, ...), custom_call_target="tpu_custom_call" | custom-call | tf_op jit(solution)/shard_map/pallas_call | solution.py:429
  49.4 1.4 %copy.11 = f32[2,16,256]{2,1,0:T(8,128)} copy(f32[2,16,256]{2,1,0:T(8,128)} %shard_map.82) | data formatting | bytes 65536
